TPU v7x, 32 devices: a whole 2x2x4 slice. The times are simulated.
32 devices in a mesh: slab: 8 (over z, x), tile: 4 (over y, core).
Axes of the slice: x: 2, y: 2, z: 4, core: 2. Of those that a mesh axis runs over, the one named last changes fastest.
Arguments:
- tiles: bfloat16 [32, 20, 256, 128], P(('slab', 'tile')), may hold values from -6 to 6
- offsets: int32 [32, 2], replicated, may hold values from -3 to 690, as said below
- fracs: int32 [32, 3], replicated, may hold values from 0 to 15
Outputs:
- joined: bfloat16 [128, 946, 128], P(('slab', 'tile'))
Inputs may be any that keep to these rules, and one draw needn't show every extreme that they name: offsets[g, 0] lies within 1 of (g // 4) * 16 - 2, and offsets[g, 1] within 4 of (g % 4) * 230, clipped to 0 .. 690; some tile reaches each end of the plane shift.
All inputs are finite; a program needn't handle non-finite values.
Results may differ from a plain program's by a relative error of at most 0.0038.
Values may be sent and summed in bfloat16 or wider, within the bound.
A program may use at most 64 MiB of HBM per device.

v0:
```python
import functools

import jax
import jax.numpy as jnp
import numpy as np
from jax import lax
from jax.experimental import pallas as pl
from jax.experimental.pallas import tpu as pltpu
from jax.sharding import PartitionSpec as P

GROUPZ = 16
MARGIN = 2
JIT = 1
STEPY = 230
JITY = 4
RY = 26
RX = 16
QUANT = 16
EDGE = MARGIN + JIT
PADY = 16
PADZ = 24

weight_floor = 0.05
MESH = pl.DeviceIdType.MESH


def ramp(length, ramp_width):
    position = np.arange(length, dtype=np.float64)
    rising = 0.5 - 0.5 * np.cos(np.pi * (position + 1.0) / (ramp_width + 1.0))
    rising = np.where(position < ramp_width, rising, 1.0)
    return np.minimum(rising, rising[::-1])


def frame_start(rank):
    if isinstance(rank, int):
        return max(rank * STEPY - JITY, 0)
    return jnp.maximum(rank * STEPY - JITY, 0)


def round_up(value, step):
    return -(-value // step) * step


def kernel(
    groups, n, per, depth, tile_rows, frame, acc_rows,
    offs_ref, fracs_ref, rampz_ref, table_ref, tile_ref, out_ref,
    raw, coef, wa, wb, blend, edge_send, edge_recv, recv, acc, rec,
    offs, fracs, rampz, table, small_sem, load_sem, es_sem, er_sem, s_sem, r_sem,
):
    g = lax.axis_index("slab")
    r = lax.axis_index("tile")
    me = g * n + r
    low = r < n // 2
    cols = raw.shape[2]
    last = n - 1

    barrier = pltpu.get_barrier_semaphore()
    for i in range(1, n):
        pl.semaphore_signal(
            barrier, inc=1, device_id=(g, lax.rem(r + i, n)), device_id_type=MESH
        )
    has_below = g > 0
    has_above = g < groups - 1

    @pl.when(has_below)
    def _():
        pl.semaphore_signal(barrier, inc=1, device_id=(g - 1, r), device_id_type=MESH)

    @pl.when(has_above)
    def _():
        pl.semaphore_signal(barrier, inc=1, device_id=(g + 1, r), device_id_type=MESH)

    smalls = [
        pltpu.make_async_copy(source, target, small_sem.at[i])
        for i, (source, target) in enumerate(
            [(offs_ref, offs), (fracs_ref, fracs), (rampz_ref, rampz), (table_ref, table)]
        )
    ]
    for small in smalls:
        small.start()
    load = pltpu.make_async_copy(tile_ref.at[0], raw.at[pl.ds(0, depth)], load_sem)
    load.start()

    def table_row(at):
        return jnp.clip(at, 0, table.shape[0] - frame)

    def rampz_at(z):
        return rampz[jnp.clip(z + PADZ, 0, rampz.shape[0] - 1)]

    for small in smalls:
        small.wait()
    corner = offs[0, me]
    shift = offs[1, me] - frame_start(r)
    fz = fracs[0, me].astype(jnp.float32) / QUANT
    fy = fracs[1, me].astype(jnp.float32) / QUANT
    fx = fracs[2, me].astype(jnp.float32) / QUANT
    row = lax.broadcasted_iota(jnp.int32, (frame, tile_rows), 0)
    col = lax.broadcasted_iota(jnp.int32, (frame, tile_rows), 1)
    behind = col - row + shift
    lerp_y = jnp.where(behind == 0, 1.0 - fy, jnp.where(behind == 1, fy, 0.0))
    coef[:, :tile_rows] = ((1.0 - fz) * lerp_y).astype(jnp.bfloat16)
    coef[:, tile_rows:] = (fz * lerp_y).astype(jnp.bfloat16)
    weight = table[pl.ds(table_row(PADY - shift), frame), :]
    lane = lax.broadcasted_iota(jnp.int32, (frame, cols), 1)
    wa[...] = weight * (1.0 - fx)
    wb[...] = jnp.where(lane < cols - 1, weight * fx, 0.0)
    raw[depth] = jnp.zeros(raw.shape[1:], raw.dtype)

    def planes(store, first, count):
        at = [jnp.clip(first + j, 0, depth - 1) for j in range(count)]
        top = jnp.concatenate([raw[z] for z in at], axis=1)
        bottom = jnp.concatenate([raw[z + 1] for z in at], axis=1)
        mixed = jnp.dot(
            coef[...], jnp.concatenate([top, bottom], axis=0),
            preferred_element_type=jnp.float32,
        )
        for j in range(count):
            part = mixed[:, j * cols : (j + 1) * cols]
            value = part * wa[...] + pltpu.roll(part, cols - 1, 1) * wb[...]
            store(j, (value * rampz_at(first + j)).astype(jnp.bfloat16))

    base = g * GROUPZ - corner

    def mirrored(owner):
        return jnp.where(low, owner, last - owner)

    def blend_owner(owner):
        def store(j, value):
            blend[owner, j] = value

        planes(store, base + owner * per, per)

    def send_owner(owner):
        @pl.when(owner != r)
        def _():
            pltpu.make_async_remote_copy(
                src_ref=blend.at[owner], dst_ref=recv.at[r],
                send_sem=s_sem.at[owner], recv_sem=r_sem.at[r],
                device_id=(g, owner), device_id_type=MESH,
            ).start()

    def send_part(owner, first, count):
        if count:
            @pl.when(owner != r)
            def _():
                part = pl.ds(first, count)
                pltpu.make_async_remote_copy(
                    src_ref=blend.at[owner, part], dst_ref=recv.at[r, part],
                    send_sem=s_sem.at[owner], recv_sem=r_sem.at[r],
                    device_id=(g, owner), device_id_type=MESH,
                ).start()

    def edge_count(o):
        o = max(o, last - o)
        return sum(1 for j in range(per) if o * per + j >= GROUPZ - EDGE)

    def send_inner(o):
        e = edge_count(o)
        upper = low if o >= n // 2 else jnp.logical_not(low)
        send_part(mirrored(o), jnp.where(upper, 0, e), per - e)

    def send_bound(o):
        e = edge_count(o)
        upper = low if o >= n // 2 else jnp.logical_not(low)
        send_part(mirrored(o), jnp.where(upper, per - e, 0), e)

    def edge_copy(side):
        return pltpu.make_async_remote_copy(
            src_ref=edge_send.at[side], dst_ref=edge_recv.at[side],
            send_sem=es_sem.at[side], recv_sem=er_sem.at[side],
            device_id=(g + 1 - 2 * side, r), device_id_type=MESH,
        )

    def sends_to(side):
        return jnp.where(side == 0, g < groups - 1, g > 0)

    def gets_from(side):
        return jnp.where(side == 0, g > 0, g < groups - 1)

    def blend_edge(side):
        def store(j, value):
            edge_send[side, j] = value

        planes(store, base + jnp.where(side == 0, GROUPZ, -EDGE), EDGE)

    def send_edge(side):
        @pl.when(sends_to(side))
        def _():
            edge_copy(side).start()

    def add_edge(side):
        @pl.when(gets_from(side))
        def _():
            for p in range(EDGE):
                q = p + jnp.where(side == 0, 0, GROUPZ - EDGE)
                owner, j = q // per, q % per
                blend[owner, j] = (
                    blend[owner, j].astype(jnp.float32)
                    + edge_recv[side, p].astype(jnp.float32)
                ).astype(jnp.bfloat16)

    def wait_edge(side):
        @pl.when(gets_from(side))
        def _():
            edge_copy(side).wait_recv()

    edge_planes = list(range(EDGE)) + list(range(GROUPZ - EDGE, GROUPZ))
    bound = sorted({q // per for q in edge_planes}, reverse=True)
    free = [o for o in range(last, -1, -1) if o not in bound]
    far_side = jnp.where(low, 1, 0)

    load.wait()
    pl.semaphore_wait(barrier, n - 1 + jnp.where(has_below, 1, 0) + jnp.where(has_above, 1, 0))
    near_side = 1 - far_side
    far_free = [o for o in free if o >= n // 2]
    far_bound = [o for o in bound if o >= n // 2]
    near_free = [o for o in free if o < n // 2]
    near_bound = [o for o in bound if o < n // 2]

    for o in far_free:
        blend_owner(mirrored(o))
        send_owner(mirrored(o))
    blend_edge(far_side)
    send_edge(far_side)
    for o in far_bound:
        blend_owner(mirrored(o))
        send_inner(o)
    for o in near_free:
        blend_owner(mirrored(o))
        send_owner(mirrored(o))
    for o in near_bound:
        blend_owner(mirrored(o))
        send_inner(o)
    blend_edge(near_side)

    rec[...] = jnp.zeros_like(rec)
    for k in range(n):
        s = frame_start(k)
        totals = [0.0] * per
        for delta in (-1, 0, 1):
            group = jnp.clip(g + delta, 0, groups - 1)
            exists = jnp.where(group == g + delta, 1.0, 0.0)
            z0 = offs[0, group * n + k]
            wy = table[pl.ds(table_row(PADY + s - offs[1, group * n + k]), frame), :]
            for j in range(per):
                z = g * GROUPZ + r * per + j - z0
                totals[j] = totals[j] + wy * (rampz_at(z) * exists)
        for j in range(per):
            rec[j, s : s + frame] = rec[j, s : s + frame] + totals[j]
    rec[...] = 1.0 / jnp.maximum(rec[...], weight_floor)

    wait_edge(far_side)
    send_edge(near_side)
    add_edge(far_side)
    for o in far_bound:
        send_bound(o)
    acc[...] = jnp.zeros_like(acc)
    wait_edge(near_side)
    add_edge(near_side)
    for o in near_bound:
        send_bound(o)

    def add(k, source):
        s = frame_start(k)
        for j in range(per):
            acc[j, pl.ds(s, frame)] = acc[j, pl.ds(s, frame)] + source[j].astype(jnp.float32)

    add(r, blend.at[r])
    for i in range(1, n):
        k = ((r // 2 + i // 2) % (n // 2)) * 2 + (r + i) % 2
        pltpu.make_async_remote_copy(
            src_ref=blend.at[r], dst_ref=recv.at[k],
            send_sem=s_sem.at[k], recv_sem=r_sem.at[k],
            device_id=(g, k), device_id_type=MESH,
        ).wait_recv()
        add(k, recv.at[k])
    rows = out_ref.shape[0]
    joined = (acc[:, :rows] * rec[:, :rows]).astype(jnp.bfloat16)
    out_ref[...] = jnp.swapaxes(joined, 0, 1)

    for i in range(1, n):
        k = lax.rem(r + i, n)
        pltpu.make_async_remote_copy(
            src_ref=blend.at[k], dst_ref=recv.at[r],
            send_sem=s_sem.at[k], recv_sem=r_sem.at[r],
            device_id=(g, k), device_id_type=MESH,
        ).wait_send()
    for side in range(2):
        @pl.when(sends_to(side))
        def _():
            edge_copy(side).wait_send()


def solution(mesh):
    groups, n = mesh.shape["slab"], mesh.shape["tile"]

    def shards(tiles, offsets, fracs):
        _, depth, tile_rows, cols = tiles.shape
        per = GROUPZ // n
        rows = (n - 1) * STEPY + tile_rows
        reach = max(
            min(k * STEPY + JITY, rows - tile_rows) + tile_rows - frame_start(k) for k in range(n)
        )
        frame = round_up(reach, 8)
        acc_rows = round_up(max(rows, frame_start(n - 1) + frame), 16)
        plane = ramp(tile_rows, RY)[:, None] * ramp(cols, RX)[None, :]
        table = np.zeros((round_up(PADY + frame + 8, 8), cols), np.float32)
        table[PADY : PADY + tile_rows] = plane
        rampz = np.zeros((depth + 2 * PADZ,), np.float32)
        rampz[PADZ : PADZ + depth] = ramp(depth, 2 * MARGIN)
        bf16, f32 = jnp.bfloat16, jnp.float32
        dma = pltpu.SemaphoreType.DMA
        joined = pl.pallas_call(
            functools.partial(kernel, groups, n, per, depth, tile_rows, frame, acc_rows),
            out_shape=pltpu.VMEM((rows, per, cols), bf16),
            in_specs=[pl.BlockSpec(memory_space=pl.ANY)] * 5,
            out_specs=pl.BlockSpec(memory_space=pltpu.VMEM),
            scratch_shapes=[
                pltpu.VMEM((depth + 1, tile_rows, cols), bf16),
                pltpu.VMEM((frame, 2 * tile_rows), bf16),
                pltpu.VMEM((frame, cols), f32),
                pltpu.VMEM((frame, cols), f32),
                pltpu.VMEM((n, per, frame, cols), bf16),
                pltpu.VMEM((2, EDGE, frame, cols), bf16),
                pltpu.VMEM((2, EDGE, frame, cols), bf16),
                pltpu.VMEM((n, per, frame, cols), bf16),
                pltpu.VMEM((per, acc_rows, cols), f32),
                pltpu.VMEM((per, acc_rows, cols), f32),
                pltpu.SMEM((offsets.shape[1], offsets.shape[0]), jnp.int32),
                pltpu.SMEM((fracs.shape[1], fracs.shape[0]), jnp.int32),
                pltpu.SMEM(rampz.shape, f32),
                pltpu.VMEM(table.shape, f32),
                dma((4,)), dma, dma((2,)), dma((2,)), dma((n,)), dma((n,)),
            ],
            compiler_params=pltpu.CompilerParams(collective_id=0, has_side_effects=True),
        )(offsets.T, fracs.T, jnp.asarray(rampz), jnp.asarray(table), tiles)
        return jnp.transpose(joined, (1, 0, 2))

    in_specs = (P(("slab", "tile"), None, None, None), P(), P())
    out_specs = P(("slab", "tile"), None, None)
    return jax.shard_map(shards, mesh=mesh, in_specs=in_specs, out_specs=out_specs, check_vma=False)
```

profile of v0, /device:TPU:0, one launch (start us, length us, event | category | flops | bytes accessed | tf_op | source)
XLA Modules:
  0.0 18.6 jit_solution(10704068812050694074)
XLA Ops:
  0.0 17.7 %shard_map.55 = bf16[946,4,128]{2,1,0:T(4,128)(2,1)S(1)} custom-call(s32[2,32]{1,0:T(2,128)} %bitcast.5, s32[3,32]{1,0:T(4,128)} %bitcast.4, f32[68]{0:T(128)} %constant.4.clone.rampz_ref, f32[288,128]{1,0:T(8,128)} %constant.5.clone.table_ref, bf16[1,20,256,128]{3,2,1,0:T(8,128)(2,1)} %tile_ref.1), custom_call_target="tpu_custom_call" | custom-call | tf_op jit(solution)/shard_map/pallas_call | solution.py:313
  17.7 0.9 %copy.7 = bf16[4,946,128]{2,0,1:T(4,128)(2,1)} copy(bf16[4,946,128]{2,0,1:T(4,128)(2,1)S(1)} %bitcast.3) | data formatting | bytes 1937408
where the time goes:
time: 18.8 us; the launch traced here: 18.6 us
  Pallas kernels  17.7 us (94%)
  local copies, waits for them, and re-layouts  0.94 us (5%)
    pallas_call x1, Pallas kernels, shards(): pl.pallas_call(functools.partial(kernel, groups, n, per, depth, tile_rows...  17.7 us
    unnamed x1, local copies, waits for them, and re-layouts  0.94 us

commit v1 on v0

v1 whole, which is shorter than its diff:
```python
import functools

import jax
import jax.numpy as jnp
import numpy as np
from jax import lax
from jax.experimental import pallas as pl
from jax.experimental.pallas import tpu as pltpu
from jax.sharding import PartitionSpec as P

GROUPZ = 16
MARGIN = 2
JIT = 1
STEPY = 230
JITY = 4
RY = 26
RX = 16
QUANT = 16
EDGE = MARGIN + JIT
PADY = 32
PADZ = 24
PIECES = 4

weight_floor = 0.05
MESH = pl.DeviceIdType.MESH


def ramp(length, ramp_width):
    position = np.arange(length, dtype=np.float64)
    rising = 0.5 - 0.5 * np.cos(np.pi * (position + 1.0) / (ramp_width + 1.0))
    rising = np.where(position < ramp_width, rising, 1.0)
    return np.minimum(rising, rising[::-1])


def round_up(value, step):
    return -(-value // step) * step


SOLO = STEPY // 8 * 8
PIECE = SOLO // PIECES


def pair_start(pair):
    if isinstance(pair, int):
        return max(2 * pair * STEPY - JITY, 0) // 8 * 8
    return jnp.maximum(2 * pair * STEPY - JITY, 0) // 8 * 8


def frame_start(rank):
    return pair_start(rank // 2) + SOLO * (rank % 2)


def kernel(
    groups, n, per, depth, tile_rows, shared,
    offs_ref, fracs_ref, rampz_ref, table_ref, tile_ref, out_ref,
    head, raw, coef, wa, wb, blend, blend_sh, own_sh, give, got,
    edge_send, edge_send_sh, edge_recv, edge_recv_sh, recv, recv_sh, rec,
    offs, fracs, rampz, table,
    small_sem, load_sem, give_sem, got_sem, es_sem, er_sem, s_sem, r_sem, above_sem,
):
    g = lax.axis_index("slab")
    r = lax.axis_index("tile")
    me = g * n + r
    low = r < n // 2
    odd = r % 2 == 1
    partner = r + 1 - 2 * (r % 2)
    cols = raw.shape[2]
    last = n - 1
    frame = SOLO + 2 * shared
    rows = out_ref.shape[0]

    barrier = pltpu.get_barrier_semaphore()
    has_below = g > 0
    has_above = g < groups - 1
    for i in range(1, n):
        pl.semaphore_signal(
            barrier, inc=1, device_id=(g, lax.rem(r + i, n)), device_id_type=MESH
        )

    @pl.when(has_above)
    def _():
        pl.semaphore_signal(barrier, inc=1, device_id=(g + 1, r), device_id_type=MESH)

    far_side = jnp.where(low, 1, 0)
    near_side = 1 - far_side

    def sends_to(side):
        return jnp.where(side == 0, g < groups - 1, g > 0)

    def gets_from(side):
        return jnp.where(side == 0, g > 0, g < groups - 1)

    gets_far = gets_from(far_side)
    gets_near = gets_from(near_side)

    def mirrored(owner):
        return jnp.where(low, owner, last - owner)

    edge_planes = list(range(EDGE)) + list(range(GROUPZ - EDGE, GROUPZ))
    bound = sorted({q // per for q in edge_planes}, reverse=True)
    free = [o for o in range(last, -1, -1) if o not in bound]
    far_free = [o for o in free if o >= n // 2]
    far_bound = [o for o in bound if o >= n // 2]
    near_free = [o for o in free if o < n // 2]
    near_bound = [o for o in bound if o < n // 2]
    far_list = far_free + far_bound

    def far_owner(i):
        return mirrored(jnp.where(gets_far, far_list[i], far_list[-1 - i]))

    smalls = [
        pltpu.make_async_copy(source, target, small_sem.at[i])
        for i, (source, target) in enumerate(
            [(offs_ref, offs), (fracs_ref, fracs), (rampz_ref, rampz), (table_ref, table)]
        )
    ]
    for small in smalls:
        small.start()
    first_owner = far_owner(0)
    head_planes = head.shape[0]
    head_start = jnp.minimum(first_owner * per + MARGIN - JIT, depth - head_planes)
    head_load = pltpu.make_async_copy(
        tile_ref.at[0, pl.ds(head_start, head_planes)], head, load_sem.at[0]
    )
    head_load.start()
    load = pltpu.make_async_copy(tile_ref.at[0], raw.at[pl.ds(0, depth)], load_sem.at[1])
    load.start()
    raw[depth] = jnp.zeros(raw.shape[1:], raw.dtype)

    def rampz_at(z):
        return rampz[jnp.clip(z + PADZ, 0, rampz.shape[0] - 1)]

    smalls[0].wait()
    smalls[1].wait()
    corner = offs[0, me]
    shift = jnp.clip(offs[1, me] - frame_start(r), 0, frame - tile_rows)
    base = g * GROUPZ - corner
    fz = fracs[0, me].astype(jnp.float32) / QUANT
    fy = fracs[1, me].astype(jnp.float32) / QUANT
    fx = fracs[2, me].astype(jnp.float32) / QUANT
    start_solo = jnp.where(odd, 2 * shared, 0)
    start_own = jnp.where(odd, shared, SOLO)
    start_give = jnp.where(odd, 0, SOLO + shared)
    parts = [(0, SOLO, start_solo), (SOLO, shared, start_own), (SOLO + shared, shared, start_give)]
    for at, count, start in parts:
        row = lax.broadcasted_iota(jnp.int32, (count, tile_rows), 0)
        col = lax.broadcasted_iota(jnp.int32, (count, tile_rows), 1)
        behind = col - row + (shift - start)
        lerp_y = jnp.where(behind == 0, 1.0 - fy, jnp.where(behind == 1, fy, 0.0))
        coef[at : at + count, :tile_rows] = ((1.0 - fz) * lerp_y).astype(jnp.bfloat16)
        coef[at : at + count, tile_rows:] = (fz * lerp_y).astype(jnp.bfloat16)
    smalls[2].wait()
    smalls[3].wait()
    for at, count, start in parts:
        weight = table[pl.ds(PADY + start - shift, count), :]
        lane = lax.broadcasted_iota(jnp.int32, (count, cols), 1)
        wa[at : at + count] = weight * (1.0 - fx)
        wb[at : at + count] = jnp.where(lane < cols - 1, weight * fx, 0.0)

    def planes(store, source, source_start, limit, first, count, lo, hi):
        at = [jnp.clip(first + j, 0, depth - 1) - source_start for j in range(count)]
        at = [jnp.clip(z, 0, limit) for z in at]
        top = jnp.concatenate([source[z] for z in at], axis=1)
        bottom = jnp.concatenate([source[z + 1] for z in at], axis=1)
        mixed = jnp.dot(
            coef[lo:hi], jnp.concatenate([top, bottom], axis=0),
            preferred_element_type=jnp.float32,
        )
        for j in range(count):
            part = mixed[:, j * cols : (j + 1) * cols]
            value = part * wa[lo:hi] + pltpu.roll(part, cols - 1, 1) * wb[lo:hi]
            store(j, value * rampz_at(first + j))

    def blend_rows(to_solo, slot, source, source_start, limit, first, count, lo, hi):
        def store(j, value):
            top = min(hi, SOLO)
            if lo < top:
                to_solo(j, lo, top, value[: top - lo].astype(jnp.bfloat16))
            if hi > SOLO:
                own_sh[slot + j] = value[SOLO - lo : SOLO + shared - lo]
                give[slot + j] = value[SOLO + shared - lo :].astype(jnp.bfloat16)

        planes(store, source, source_start, limit, first, count, lo, hi)

    def blend_owner(owner, lo=0, hi=frame, from_head=False):
        def to_solo(j, a, b, value):
            blend[owner, j, a:b] = value

        first = base + owner * per
        if from_head:
            blend_rows(
                to_solo, owner * per, head, head_start, head_planes - 2, first, per, lo, hi
            )
        else:
            blend_rows(to_solo, owner * per, raw, 0, depth - 1, first, per, lo, hi)

    def edge_slot(side):
        return GROUPZ + side * EDGE

    def blend_edge(side):
        def to_solo(j, a, b, value):
            edge_send[side, j, a:b] = value

        first = base + jnp.where(side == 0, GROUPZ, -EDGE)
        blend_rows(to_solo, edge_slot(side), raw, 0, depth - 1, first, EDGE, 0, frame)

    def swap_copy(at, slot, count):
        part = pl.ds(slot, count)
        return pltpu.make_async_remote_copy(
            src_ref=give.at[part], dst_ref=got.at[part],
            send_sem=give_sem.at[at], recv_sem=got_sem.at[at],
            device_id=(g, partner), device_id_type=MESH,
        )

    def swap_owner(owner):
        return swap_copy(owner, owner * per, per)

    def swap_edge(side):
        return swap_copy(n + side, edge_slot(side), EDGE)

    def join_owner(owner):
        swap_owner(owner).wait_recv()
        for j in range(per):
            slot = owner * per + j
            blend_sh[owner, j] = (own_sh[slot] + got[slot].astype(jnp.float32)).astype(jnp.bfloat16)

    def join_edge(side):
        swap_edge(side).wait_recv()
        for p in range(EDGE):
            slot = edge_slot(side) + p
            edge_send_sh[side, p] = (own_sh[slot] + got[slot].astype(jnp.float32)).astype(
                jnp.bfloat16
            )

    def of(solo, sh, at, i):
        if i == PIECES:
            return sh.at[at]
        return solo.at[at, :, pl.ds(i * PIECE, PIECE)]

    def owner_copy(owner, source, i):
        return pltpu.make_async_remote_copy(
            src_ref=of(blend, blend_sh, owner, i), dst_ref=of(recv, recv_sh, source, i),
            send_sem=s_sem.at[owner, i], recv_sem=r_sem.at[source, i],
            device_id=(g, owner), device_id_type=MESH,
        )

    def own_copy(i):
        return pltpu.make_async_copy(
            of(blend, blend_sh, r, i), of(recv, recv_sh, r, i), r_sem.at[r, i]
        )

    def send(owner, i, when=True):
        @pl.when(jnp.logical_and(when, owner != r))
        def _():
            owner_copy(owner, r, i).start()

        @pl.when(jnp.logical_and(when, owner == r))
        def _():
            own_copy(i).start()

    def edge_copy(side, i):
        return pltpu.make_async_remote_copy(
            src_ref=of(edge_send, edge_send_sh, side, i),
            dst_ref=of(edge_recv, edge_recv_sh, side, i),
            send_sem=es_sem.at[side, i], recv_sem=er_sem.at[side, i],
            device_id=(g + 1 - 2 * side, r), device_id_type=MESH,
        )

    def send_edge(side, i):
        @pl.when(sends_to(side))
        def _():
            edge_copy(side, i).start()

    def add_edge(side, i):
        edge_copy(side, i).wait_recv()
        for p in range(EDGE):
            q = p + jnp.where(side == 0, 0, GROUPZ - EDGE)
            owner, j = q // per, q % per
            if i == PIECES:
                blend_sh[owner, j] = (
                    blend_sh[owner, j].astype(jnp.float32)
                    + edge_recv_sh[side, p].astype(jnp.float32)
                ).astype(jnp.bfloat16)
            else:
                a, b = i * PIECE, (i + 1) * PIECE
                blend[owner, j, a:b] = (
                    blend[owner, j, a:b].astype(jnp.float32)
                    + edge_recv[side, p, a:b].astype(jnp.float32)
                ).astype(jnp.bfloat16)

    head_load.wait()
    blend_owner(first_owner, 0, PIECE, True)
    pl.semaphore_wait(barrier, n - 1 + jnp.where(has_below, 1, 0))
    first_free = len(far_free) > 0
    first_when = True if first_free else jnp.logical_not(gets_far)
    send(first_owner, 0, first_when)

    @pl.when(has_below)
    def _():
        pl.semaphore_signal(above_sem, inc=1, device_id=(g - 1, r), device_id_type=MESH)

    blend_owner(first_owner, PIECE, frame, True)
    for i in range(1, PIECES):
        send(first_owner, i, first_when)
    swap_owner(first_owner).start()

    load.wait()
    blend_edge(far_side)

    @pl.when(jnp.logical_and(has_above, jnp.logical_not(low)))
    def _():
        pl.semaphore_wait(above_sem, 1)

    for i in range(PIECES):
        send_edge(far_side, i)
    swap_edge(far_side).start()

    for at in range(1, len(far_list)):
        owner = far_owner(at)
        blend_owner(owner)
        for i in range(PIECES):
            send(owner, i, True if at < len(far_free) else jnp.logical_not(gets_far))
        swap_owner(owner).start()
    join_edge(far_side)
    send_edge(far_side, PIECES)
    for at in range(len(far_list)):
        owner = far_owner(at)
        join_owner(owner)
        send(owner, PIECES, True if at < len(far_free) else jnp.logical_not(gets_far))

    blend_edge(near_side)

    @pl.when(jnp.logical_and(has_above, low))
    def _():
        pl.semaphore_wait(above_sem, 1)

    for i in range(PIECES):
        send_edge(near_side, i)
    swap_edge(near_side).start()
    for o in near_free + near_bound:
        owner = mirrored(o)
        blend_owner(owner)
        for i in range(PIECES):
            send(owner, i, True if o in near_free else jnp.logical_not(gets_near))
        swap_owner(owner).start()
    join_edge(near_side)
    send_edge(near_side, PIECES)
    for o in near_free + near_bound:
        owner = mirrored(o)
        join_owner(owner)
        send(owner, PIECES, True if o in near_free else jnp.logical_not(gets_near))

    rec[...] = jnp.zeros_like(rec)
    for k in range(n):
        s = frame_start(k)
        totals = [0.0] * per
        for delta in (-1, 0, 1):
            group = jnp.clip(g + delta, 0, groups - 1)
            exists = jnp.where(group == g + delta, 1.0, 0.0)
            z0 = offs[0, group * n + k]
            ahead = jnp.clip(offs[1, group * n + k] - s, 0, frame - tile_rows)
            wy = table[pl.ds(PADY - ahead, frame), :]
            for j in range(per):
                z = g * GROUPZ + r * per + j - z0
                totals[j] = totals[j] + wy * (rampz_at(z) * exists)
        for j in range(per):
            rec[j, s : s + frame] = rec[j, s : s + frame] + totals[j]
    rec[...] = 1.0 / jnp.maximum(rec[...], weight_floor)

    @pl.when(gets_far)
    def _():
        for i in range(PIECES + 1):
            add_edge(far_side, i)
            for o in far_bound:
                send(mirrored(o), i)

    @pl.when(gets_near)
    def _():
        for i in range(PIECES + 1):
            add_edge(near_side, i)
            for o in near_bound:
                send(mirrored(o), i)

    def span(k, i):
        at = pair_start(k // 2) + (k % 2) * (SOLO + 2 * shared)
        if i < PIECES:
            return at + i * PIECE, at + (i + 1) * PIECE
        at = pair_start(k // 2) + SOLO + (k % 2) * shared
        return at, at + shared

    def taken(k, i, a, b):
        lo, _ = span(k, i)
        if i < PIECES:
            lo -= i * PIECE
            return recv[k, :, a - lo : b - lo].astype(jnp.float32)
        return recv_sh[k, :, a - lo : b - lo].astype(jnp.float32)

    every = [(k, i) for k in range(n) for i in range(PIECES + 1)]
    cuts = sorted({min(end, rows) for piece in every for end in span(*piece)})

    def finish(order):
        here = []
        left = [
            (a, b, [p for p in every if span(*p)[0] < b and span(*p)[1] > a])
            for a, b in zip(cuts[:-1], cuts[1:])
        ]
        for k, i in order:
            owner_copy(r, k, i).wait_recv()
            here.append((k, i))
            ready = [item for item in left if all(p in here for p in item[2])]
            left = [item for item in left if item not in ready]
            for a, b, pieces in ready:
                total = sum(taken(*p, a, b) for p in pieces)
                value = (total * rec[:, a:b]).astype(jnp.bfloat16)
                out_ref[a:b] = jnp.swapaxes(value, 0, 1)

    for is_low in (True, False):
        near = [k for k in range(n) if (k < n // 2) == is_low]
        far = [k for k in range(n) if (k < n // 2) != is_low]
        order = [(k, i) for i in range(PIECES - 1) for k in far]
        order += [(k, i) for i in range(PIECES + 1) for k in near]
        order += [(k, i) for i in (PIECES - 1, PIECES) for k in far]

        @pl.when(low == is_low)
        def _():
            finish(order)

    for o in range(n):
        swap_owner(o).wait_send()

        @pl.when(r != o)
        def _():
            for i in range(PIECES + 1):
                owner_copy(o, r, i).wait_send()

    for side in range(2):
        swap_edge(side).wait_send()

        @pl.when(sends_to(side))
        def _():
            for i in range(PIECES + 1):
                edge_copy(side, i).wait_send()


def solution(mesh):
    groups, n = mesh.shape["slab"], mesh.shape["tile"]

    def shards(tiles, offsets, fracs):
        _, depth, tile_rows, cols = tiles.shape
        per = GROUPZ // n
        rows = (n - 1) * STEPY + tile_rows
        reach = max(
            min(k * STEPY + JITY, rows - tile_rows) + tile_rows - frame_start(k) for k in range(n)
        )
        shared = round_up(max(reach - SOLO, 16), 16) // 2
        frame = SOLO + 2 * shared
        acc_rows = round_up(max(rows, frame_start(n - 1) + frame), 16)
        head = per + 2 * JIT + 1
        plane = ramp(tile_rows, RY)[:, None] * ramp(cols, RX)[None, :]
        table = np.zeros((round_up(PADY + frame + 8, 8), cols), np.float32)
        table[PADY : PADY + tile_rows] = plane
        rampz = np.zeros((depth + 2 * PADZ,), np.float32)
        rampz[PADZ : PADZ + depth] = ramp(depth, 2 * MARGIN)
        bf16, f32 = jnp.bfloat16, jnp.float32
        dma = pltpu.SemaphoreType.DMA
        slots = GROUPZ + 2 * EDGE
        joined = pl.pallas_call(
            functools.partial(kernel, groups, n, per, depth, tile_rows, shared),
            out_shape=pltpu.VMEM((rows, per, cols), bf16),
            in_specs=[pl.BlockSpec(memory_space=pl.ANY)] * 5,
            out_specs=pl.BlockSpec(memory_space=pltpu.VMEM),
            scratch_shapes=[
                pltpu.VMEM((head, tile_rows, cols), bf16),
                pltpu.VMEM((depth + 1, tile_rows, cols), bf16),
                pltpu.VMEM((frame, 2 * tile_rows), bf16),
                pltpu.VMEM((frame, cols), f32),
                pltpu.VMEM((frame, cols), f32),
                pltpu.VMEM((n, per, SOLO, cols), bf16),
                pltpu.VMEM((n, per, shared, cols), bf16),
                pltpu.VMEM((slots, shared, cols), f32),
                pltpu.VMEM((slots, shared, cols), bf16),
                pltpu.VMEM((slots, shared, cols), bf16),
                pltpu.VMEM((2, EDGE, SOLO, cols), bf16),
                pltpu.VMEM((2, EDGE, shared, cols), bf16),
                pltpu.VMEM((2, EDGE, SOLO, cols), bf16),
                pltpu.VMEM((2, EDGE, shared, cols), bf16),
                pltpu.VMEM((n, per, SOLO, cols), bf16),
                pltpu.VMEM((n, per, shared, cols), bf16),
                pltpu.VMEM((per, acc_rows, cols), f32),
                pltpu.SMEM((offsets.shape[1], offsets.shape[0]), jnp.int32),
                pltpu.SMEM((fracs.shape[1], fracs.shape[0]), jnp.int32),
                pltpu.SMEM(rampz.shape, f32),
                pltpu.VMEM(table.shape, f32),
                dma((4,)), dma((2,)), dma((n + 2,)), dma((n + 2,)),
                dma((2, PIECES + 1)), dma((2, PIECES + 1)),
                dma((n, PIECES + 1)), dma((n, PIECES + 1)),
                pltpu.SemaphoreType.REGULAR,
            ],
            compiler_params=pltpu.CompilerParams(collective_id=0, has_side_effects=True),
        )(offsets.T, fracs.T, jnp.asarray(rampz), jnp.asarray(table), tiles)
        return jnp.transpose(joined, (1, 0, 2))

    in_specs = (P(("slab", "tile"), None, None, None), P(), P())
    out_specs = P(("slab", "tile"), None, None)
    return jax.shard_map(shards, mesh=mesh, in_specs=in_specs, out_specs=out_specs, check_vma=False)
```

time: 18.8 us -> 18.3 us (0.973)
  the two profiles are of different devices: /device:TPU:0 before, /device:TPU:13 now
where the time goes in v1:
time: 18.3 us; the launch traced here: 18.2 us
  Pallas kernels  17.2 us (94%)
  local copies, waits for them, and re-layouts  0.94 us (5%)
    pallas_call x1, Pallas kernels, shards(): pl.pallas_call(functools.partial(kernel, groups, n, per, depth, tile_rows...  17.2 us
    unnamed x1, local copies, waits for them, and re-layouts  0.94 us

profile of v1, /device:TPU:13, one launch (start us, length us, event | category | flops | bytes accessed | tf_op | source)
XLA Modules:
  0.0 18.2 jit_solution(16235857025307106984)
XLA Ops:
  0.0 17.2 %shard_map.55 = bf16[946,4,128]{2,1,0:T(4,128)(2,1)S(1)} custom-call(s32[2,32]{1,0:T(2,128)} %bitcast.5, s32[3,32]{1,0:T(4,128)} %bitcast.4, f32[68]{0:T(128)} %constant.4.clone.rampz_ref, f32[312,128]{1,0:T(8,128)} %constant.5.clone.table_ref, bf16[1,20,256,128]{3,2,1,0:T(8,128)(2,1)} %tile_ref.1), custom_call_target="tpu_custom_call" | custom-call | tf_op jit(solution)/shard_map/pallas_call | solution.py:467
  17.2 0.9 %copy.7 = bf16[4,946,128]{2,0,1:T(4,128)(2,1)} copy(bf16[4,946,128]{2,0,1:T(4,128)(2,1)S(1)} %bitcast.3) | data formatting | bytes 1937408

commit v2 on v1

v2 whole, which is shorter than its diff:
```python
import functools

import jax
import jax.numpy as jnp
import numpy as np
from jax import lax
from jax.experimental import pallas as pl
from jax.experimental.pallas import tpu as pltpu
from jax.sharding import PartitionSpec as P

GROUPZ = 16
MARGIN = 2
JIT = 1
STEPY = 230
JITY = 4
RY = 26
RX = 16
QUANT = 16
EDGE = MARGIN + JIT
PADY = 32
PADZ = 24
PIECES = 4

weight_floor = 0.05
MESH = pl.DeviceIdType.MESH


def ramp(length, ramp_width):
    position = np.arange(length, dtype=np.float64)
    rising = 0.5 - 0.5 * np.cos(np.pi * (position + 1.0) / (ramp_width + 1.0))
    rising = np.where(position < ramp_width, rising, 1.0)
    return np.minimum(rising, rising[::-1])


def round_up(value, step):
    return -(-value // step) * step


SOLO = STEPY // 8 * 8


def pair_start(pair):
    if isinstance(pair, int):
        return max(2 * pair * STEPY - JITY, 0) // 8 * 8
    return jnp.maximum(2 * pair * STEPY - JITY, 0) // 8 * 8


def frame_start(rank):
    return pair_start(rank // 2) + SOLO * (rank % 2)


def kernel(
    groups, n, per, depth, tile_rows, shared,
    offs_ref, fracs_ref, rampz_ref, table_ref, tile_ref, out_ref,
    head, raw, coef, wa, wb, blend, own_sh, give, got,
    edge_send, far_recv, near_recv, recv, rec,
    offs, fracs, rampz, table,
    small_sem, load_sem, give_sem, got_sem, es_sem, far_sem, near_sem, s_sem, r_sem,
    above_sem, below_sem,
):
    g = lax.axis_index("slab")
    r = lax.axis_index("tile")
    me = g * n + r
    chip = r // 2
    pairs = n // 2
    low = r < n // 2
    high = jnp.logical_not(low)
    odd = r % 2 == 1
    partner = r + 1 - 2 * (r % 2)
    cols = raw.shape[2]
    last = n - 1
    frame = SOLO + 2 * shared
    half = SOLO + shared
    rows = out_ref.shape[0]
    steps = half // 8
    cut = [steps * i // PIECES * 8 for i in range(PIECES + 1)]
    direct = pairs == 2

    barrier = pltpu.get_barrier_semaphore()
    has_below = g > 0
    has_above = g < groups - 1
    for i in range(1, n):
        pl.semaphore_signal(
            barrier, inc=1, device_id=(g, lax.rem(r + i, n)), device_id_type=MESH
        )

    @pl.when(has_above)
    def _():
        pl.semaphore_signal(barrier, inc=1, device_id=(g + 1, r), device_id_type=MESH)

    far_side = jnp.where(low, 1, 0)
    near_side = 1 - far_side

    def sends_to(side):
        return jnp.where(side == 0, g < groups - 1, g > 0)

    def gets_from(side):
        return jnp.where(side == 0, g > 0, g < groups - 1)

    gets_far = gets_from(far_side)
    gets_near = gets_from(near_side)

    def mirrored(owner):
        return jnp.where(low, owner, last - owner)

    edge_planes = list(range(EDGE)) + list(range(GROUPZ - EDGE, GROUPZ))
    bound = sorted({q // per for q in edge_planes}, reverse=True)
    free = [o for o in range(last, -1, -1) if o not in bound]
    far_free = [o for o in free if o >= n // 2]
    far_bound = [o for o in bound if o >= n // 2]
    near_free = [o for o in free if o < n // 2]
    near_bound = [o for o in bound if o < n // 2]
    far_list = far_free + far_bound
    near_list = near_free + near_bound
    near_owner = mirrored(near_bound[-1])
    takes_near = jnp.logical_and(gets_near, r == near_owner)

    def far_owner(i):
        return mirrored(jnp.where(gets_far, far_list[i], far_list[-1 - i]))

    smalls = [
        pltpu.make_async_copy(source, target, small_sem.at[i])
        for i, (source, target) in enumerate(
            [(offs_ref, offs), (fracs_ref, fracs), (rampz_ref, rampz), (table_ref, table)]
        )
    ]
    for small in smalls:
        small.start()
    first_owner = far_owner(0)
    head_planes = head.shape[0]
    head_start = jnp.minimum(first_owner * per + MARGIN - JIT, depth - head_planes)
    head_load = pltpu.make_async_copy(
        tile_ref.at[0, pl.ds(head_start, head_planes)], head, load_sem.at[0]
    )
    head_load.start()
    load = pltpu.make_async_copy(tile_ref.at[0], raw.at[pl.ds(0, depth)], load_sem.at[1])
    load.start()
    raw[depth] = jnp.zeros(raw.shape[1:], raw.dtype)

    def rampz_at(z):
        return rampz[jnp.clip(z + PADZ, 0, rampz.shape[0] - 1)]

    smalls[0].wait()
    smalls[1].wait()
    corner = offs[0, me]
    shift = jnp.clip(offs[1, me] - frame_start(r), 0, frame - tile_rows)
    base = g * GROUPZ - corner
    fz = fracs[0, me].astype(jnp.float32) / QUANT
    fy = fracs[1, me].astype(jnp.float32) / QUANT
    fx = fracs[2, me].astype(jnp.float32) / QUANT
    start_solo = jnp.where(odd, 2 * shared, 0)
    start_own = jnp.where(odd, shared, SOLO)
    start_give = jnp.where(odd, 0, half)
    parts = [(0, SOLO, start_solo), (SOLO, shared, start_own), (half, shared, start_give)]
    for at, count, start in parts:
        row = lax.broadcasted_iota(jnp.int32, (count, tile_rows), 0)
        col = lax.broadcasted_iota(jnp.int32, (count, tile_rows), 1)
        behind = col - row + (shift - start)
        lerp_y = jnp.where(behind == 0, 1.0 - fy, jnp.where(behind == 1, fy, 0.0))
        coef[at : at + count, :tile_rows] = ((1.0 - fz) * lerp_y).astype(jnp.bfloat16)
        coef[at : at + count, tile_rows:] = (fz * lerp_y).astype(jnp.bfloat16)
    smalls[2].wait()
    smalls[3].wait()
    for at, count, start in parts:
        weight = table[pl.ds(PADY + start - shift, count), :]
        lane = lax.broadcasted_iota(jnp.int32, (count, cols), 1)
        wa[at : at + count] = weight * (1.0 - fx)
        wb[at : at + count] = jnp.where(lane < cols - 1, weight * fx, 0.0)

    def planes(store, source, source_start, limit, first, count, lo, hi):
        at = [jnp.clip(first + j, 0, depth - 1) - source_start for j in range(count)]
        at = [jnp.clip(z, 0, limit) for z in at]
        top = jnp.concatenate([source[z] for z in at], axis=1)
        bottom = jnp.concatenate([source[z + 1] for z in at], axis=1)
        mixed = jnp.dot(
            coef[lo:hi], jnp.concatenate([top, bottom], axis=0),
            preferred_element_type=jnp.float32,
        )
        for j in range(count):
            part = mixed[:, j * cols : (j + 1) * cols]
            value = part * wa[lo:hi] + pltpu.roll(part, cols - 1, 1) * wb[lo:hi]
            store(j, value * rampz_at(first + j))

    def blend_rows(target, at, slot, where_from, first, count, lo, hi):
        def store(j, value):
            top = min(hi, SOLO)
            if lo < top:
                target[at, j, lo:top] = value[: top - lo].astype(jnp.bfloat16)
            if hi > SOLO:
                own_sh[slot + j] = value[SOLO - lo : half - lo]
                give[slot + j] = value[half - lo :].astype(jnp.bfloat16)

        planes(store, *where_from, first, count, lo, hi)

    whole = (raw, 0, depth - 1)

    def blend_owner(owner, lo=0, hi=frame, where_from=whole):
        blend_rows(blend, owner, owner * per, where_from, base + owner * per, per, lo, hi)

    def edge_slot(side):
        return GROUPZ + side * EDGE

    def blend_edge(side):
        first = base + jnp.where(side == 0, GROUPZ, -EDGE)
        blend_rows(edge_send, side, edge_slot(side), whole, first, EDGE, 0, frame)

    def swap_copy(slot, count, at):
        part = pl.ds(slot, count)
        return pltpu.make_async_remote_copy(
            src_ref=give.at[part], dst_ref=got.at[part],
            send_sem=give_sem, recv_sem=got_sem.at[at],
            device_id=(g, partner), device_id_type=MESH,
        )

    def joined_rows(slot):
        return (own_sh[slot] + got[slot].astype(jnp.float32)).astype(jnp.bfloat16)

    def join_owner(owner):
        for j in range(per):
            blend[owner, j, SOLO:half] = joined_rows(owner * per + j)

    def join_edge(side):
        for p in range(EDGE):
            edge_send[side, p, SOLO:half] = joined_rows(edge_slot(side) + p)

    def rows_of(i):
        return pl.ds(cut[i], cut[i + 1] - cut[i])

    def came(source_chip, i):
        away = lax.rem(source_chip - chip + pairs, pairs)
        return jnp.where(away == 0, 0, 1 + (away - 1) * PIECES + i)

    def send(owner, i, when=True):
        there = owner // 2
        away = lax.rem(chip - there + pairs, pairs)
        at = jnp.where(away == 0, 0, 1 + (away - 1) * PIECES + i)

        @pl.when(jnp.logical_and(when, owner != r))
        def _():
            pltpu.make_async_remote_copy(
                src_ref=blend.at[owner, :, rows_of(i)], dst_ref=recv.at[r, :, rows_of(i)],
                send_sem=s_sem, recv_sem=r_sem.at[at],
                device_id=(g, owner), device_id_type=MESH,
            ).start()

        @pl.when(jnp.logical_and(when, owner == r))
        def _():
            pltpu.make_async_copy(
                blend.at[owner, :, rows_of(i)], recv.at[r, :, rows_of(i)], r_sem.at[at]
            ).start()

    def await_far(source_chip, i):
        part = recv.at[pl.ds(2 * source_chip, 2), :, rows_of(i)]
        pltpu.make_async_copy(part, part, r_sem.at[came(source_chip, i)]).wait()

    def await_own():
        part = recv.at[pl.ds(2 * chip, 2)]
        pltpu.make_async_copy(part, part, r_sem.at[0]).wait()

    def send_far(i):
        @pl.when(sends_to(far_side))
        def _():
            pltpu.make_async_remote_copy(
                src_ref=edge_send.at[far_side, :, rows_of(i)], dst_ref=far_recv.at[:, rows_of(i)],
                send_sem=es_sem.at[0], recv_sem=far_sem.at[i],
                device_id=(g + 1 - 2 * far_side, r), device_id_type=MESH,
            ).start()

    near_slot = r % 2 if direct else 0
    near_target = near_owner if direct else r

    def send_near(i):
        @pl.when(sends_to(near_side))
        def _():
            pltpu.make_async_remote_copy(
                src_ref=edge_send.at[near_side, :, rows_of(i)],
                dst_ref=near_recv.at[near_slot, :, rows_of(i)],
                send_sem=es_sem.at[1], recv_sem=near_sem.at[i],
                device_id=(g + 1 - 2 * near_side, near_target), device_id_type=MESH,
            ).start()

    def await_piece(part, sem):
        pltpu.make_async_copy(part, part, sem).wait()

    def add_edge(side, source, i):
        for p in range(EDGE):
            q = p + jnp.where(side == 0, 0, GROUPZ - EDGE)
            owner, j = q // per, q % per
            a, b = cut[i], cut[i + 1]
            blend[owner, j, a:b] = (
                blend[owner, j, a:b].astype(jnp.float32) + source[p, a:b].astype(jnp.float32)
            ).astype(jnp.bfloat16)

    near_head = (head, head_start, head_planes - 2)
    head_load.wait()
    blend_owner(first_owner, 0, cut[1], near_head)
    pl.semaphore_wait(barrier, n - 1 + jnp.where(has_below, 1, 0))
    not_far = jnp.logical_not(gets_far)
    send(first_owner, 0, True if far_free else not_far)

    @pl.when(has_below)
    def _():
        pl.semaphore_signal(above_sem, inc=1, device_id=(g - 1, r), device_id_type=MESH)

    blend_owner(first_owner, cut[1], frame, near_head)
    for i in range(1, PIECES - 1):
        send(first_owner, i, True if far_free else not_far)
    swap_copy(first_owner * per, per, 0).start()

    load.wait()
    blend_edge(far_side)
    swap_copy(edge_slot(far_side), EDGE, 0).start()

    @pl.when(low)
    def _():
        for i in range(PIECES - 1):
            send_far(i)

    for at in range(1, len(far_list)):
        owner = far_owner(at)
        blend_owner(owner)
        swap_copy(owner * per, per, 1).start()

    @pl.when(jnp.logical_and(has_above, high))
    def _():
        pl.semaphore_wait(above_sem, 1)
        if direct:
            pl.semaphore_signal(below_sem, inc=1, device_id=(g + 1, r), device_id_type=MESH)
        for i in range(PIECES - 1):
            send_far(i)

    await_piece(got.at[pl.ds(0, per + EDGE)], got_sem.at[0])
    join_owner(first_owner)
    send(first_owner, PIECES - 1, True if far_free else not_far)
    join_edge(far_side)
    send_far(PIECES - 1)
    for at in range(1, len(far_list)):
        owner = far_owner(at)
        for i in range(PIECES - 1):
            send(owner, i, True if at < len(far_free) else not_far)

    for o in near_list:
        owner = mirrored(o)
        blend_owner(owner)
        swap_copy(owner * per, per, 1).start()
    blend_edge(near_side)
    swap_copy(edge_slot(near_side), EDGE, 1).start()
    if direct:
        @pl.when(jnp.logical_not(takes_near))
        def _():
            near_recv[...] = jnp.zeros_like(near_recv)

    await_piece(got.at[pl.ds(0, GROUPZ - per + EDGE)], got_sem.at[1])
    for at in range(1, len(far_list)):
        owner = far_owner(at)
        join_owner(owner)
        send(owner, PIECES - 1, True if at < len(far_free) else not_far)
    for o in near_list:
        owner = mirrored(o)
        join_owner(owner)
        for i in range(PIECES):
            send(owner, i, True if direct or o in near_free else jnp.logical_not(gets_near))
    join_edge(near_side)

    rec[...] = jnp.zeros_like(rec)
    for k in range(n):
        s = frame_start(k)
        totals = [0.0] * per
        for delta in (-1, 0, 1):
            group = jnp.clip(g + delta, 0, groups - 1)
            exists = jnp.where(group == g + delta, 1.0, 0.0)
            z0 = offs[0, group * n + k]
            ahead = jnp.clip(offs[1, group * n + k] - s, 0, frame - tile_rows)
            wy = table[pl.ds(PADY - ahead, frame), :]
            for j in range(per):
                z = g * GROUPZ + r * per + j - z0
                totals[j] = totals[j] + wy * (rampz_at(z) * exists)
        for j in range(per):
            rec[j, s : s + frame] = rec[j, s : s + frame] + totals[j]
    rec[...] = 1.0 / jnp.maximum(rec[...], weight_floor)

    @pl.when(jnp.logical_and(has_above, low))
    def _():
        pl.semaphore_wait(above_sem, 1)

    if direct:
        @pl.when(jnp.logical_and(has_below, high))
        def _():
            pl.semaphore_wait(below_sem, 1)

    for i in range(PIECES):
        @pl.when(gets_far)
        def _():
            await_piece(far_recv.at[:, rows_of(i)], far_sem.at[i])
            add_edge(far_side, far_recv, i)
            for o in far_bound:
                send(mirrored(o), i)

        send_near(i)

    if not direct:
        @pl.when(gets_near)
        def _():
            for i in range(PIECES):
                await_piece(near_recv.at[0, :, rows_of(i)], near_sem.at[i])
                add_edge(near_side, near_recv.at[0], i)
                for o in near_bound:
                    send(mirrored(o), i)

    def spans(k, i):
        solo_at = pair_start(k // 2) + (k % 2) * (SOLO + 2 * shared)
        shared_at = pair_start(k // 2) + SOLO + (k % 2) * shared
        a, b = cut[i], cut[i + 1]
        found = [(solo_at + a, solo_at + min(b, SOLO), solo_at)] if a < SOLO else []
        if b > SOLO:
            a = max(a, SOLO)
            found.append((shared_at + a - SOLO, shared_at + b - SOLO, shared_at - SOLO))
        return found

    segments = [(k, i, *span) for k in range(n) for i in range(PIECES) for span in spans(k, i)]
    marks = sorted({min(end, rows) for item in segments for end in item[2:4]})
    intervals = [
        (a, b, [(k, i, at) for k, i, lo, hi, at in segments if lo < b and hi > a])
        for a, b in zip(marks[:-1], marks[1:])
    ]

    def finish(a, b, pieces, own=None, first=0):
        total = 0.0
        for k, i, at in pieces:
            total = total + recv[k, :, a - at : b - at].astype(jnp.float32)
            if k // 2 == own:
                edge = near_recv[k % 2, :, a - at : b - at].astype(jnp.float32)
                blank = [jnp.zeros((count, b - a, cols), jnp.float32) for count in (first, per - EDGE - first)]
                kept = [part for part in (blank[0], edge, blank[1]) if part.shape[0]]
                total = total + jnp.concatenate(kept, axis=0)
        value = (total * rec[:, a:b]).astype(jnp.bfloat16)
        out_ref[a:b] = jnp.swapaxes(value, 0, 1)

    if direct:
        for own in range(2):
            @pl.when(chip == own)
            def _():
                left = list(intervals)
                here = set()
                await_own()
                for i in range(PIECES):
                    @pl.when(takes_near)
                    def _():
                        await_piece(near_recv.at[:, :, rows_of(i)], near_sem.at[i])

                    for source in (own, 1 - own):
                        if source != own:
                            await_far(source, i)
                        here |= {(2 * source, i), (2 * source + 1, i)}
                        for item in list(left):
                            if all((k, j) in here for k, j, _ in item[2]):
                                left.remove(item)
                                finish(*item, own, 0 if own == 0 else per - EDGE)
    else:
        await_own()
        for away in range(1, pairs):
            for i in range(PIECES):
                await_far(lax.rem(chip + away, pairs), i)
        for item in intervals:
            finish(*item)

    def await_sent(part, sem):
        pltpu.make_async_copy(part, part, sem).wait()

    await_sent(give, give_sem)
    await_sent(blend.at[pl.ds(0, n - 1)], s_sem)
    for at, side in enumerate((far_side, near_side)):
        @pl.when(sends_to(side))
        def _():
            await_sent(far_recv, es_sem.at[at])


def solution(mesh):
    groups, n = mesh.shape["slab"], mesh.shape["tile"]

    def shards(tiles, offsets, fracs):
        _, depth, tile_rows, cols = tiles.shape
        per = GROUPZ // n
        rows = (n - 1) * STEPY + tile_rows
        reach = max(
            min(k * STEPY + JITY, rows - tile_rows) + tile_rows - frame_start(k) for k in range(n)
        )
        shared = round_up(max(reach - SOLO, 16), 16) // 2
        frame, half = SOLO + 2 * shared, SOLO + shared
        acc_rows = round_up(max(rows, frame_start(n - 1) + frame), 16)
        head = per + 2 * JIT + 1
        plane = ramp(tile_rows, RY)[:, None] * ramp(cols, RX)[None, :]
        table = np.zeros((round_up(PADY + frame + 8, 8), cols), np.float32)
        table[PADY : PADY + tile_rows] = plane
        rampz = np.zeros((depth + 2 * PADZ,), np.float32)
        rampz[PADZ : PADZ + depth] = ramp(depth, 2 * MARGIN)
        bf16, f32 = jnp.bfloat16, jnp.float32
        dma, signal = pltpu.SemaphoreType.DMA, pltpu.SemaphoreType.REGULAR
        slots = GROUPZ + 2 * EDGE
        joined = pl.pallas_call(
            functools.partial(kernel, groups, n, per, depth, tile_rows, shared),
            out_shape=pltpu.VMEM((rows, per, cols), bf16),
            in_specs=[pl.BlockSpec(memory_space=pl.ANY)] * 5,
            out_specs=pl.BlockSpec(memory_space=pltpu.VMEM),
            scratch_shapes=[
                pltpu.VMEM((head, tile_rows, cols), bf16),
                pltpu.VMEM((depth + 1, tile_rows, cols), bf16),
                pltpu.VMEM((frame, 2 * tile_rows), bf16),
                pltpu.VMEM((frame, cols), f32),
                pltpu.VMEM((frame, cols), f32),
                pltpu.VMEM((n, per, half, cols), bf16),
                pltpu.VMEM((slots, shared, cols), f32),
                pltpu.VMEM((slots, shared, cols), bf16),
                pltpu.VMEM((slots, shared, cols), bf16),
                pltpu.VMEM((2, EDGE, half, cols), bf16),
                pltpu.VMEM((EDGE, half, cols), bf16),
                pltpu.VMEM((2, EDGE, half, cols), bf16),
                pltpu.VMEM((n, per, half, cols), bf16),
                pltpu.VMEM((per, acc_rows, cols), f32),
                pltpu.SMEM((offsets.shape[1], offsets.shape[0]), jnp.int32),
                pltpu.SMEM((fracs.shape[1], fracs.shape[0]), jnp.int32),
                pltpu.SMEM(rampz.shape, f32),
                pltpu.VMEM(table.shape, f32),
                dma((4,)), dma((2,)), dma, dma((2,)), dma((2,)),
                dma((PIECES,)), dma((PIECES,)), dma, dma(((n // 2 - 1) * PIECES + 1,)),
                signal, signal,
            ],
            compiler_params=pltpu.CompilerParams(collective_id=0, has_side_effects=True),
        )(offsets.T, fracs.T, jnp.asarray(rampz), jnp.asarray(table), tiles)
        return jnp.transpose(joined, (1, 0, 2))

    in_specs = (P(("slab", "tile"), None, None, None), P(), P())
    out_specs = P(("slab", "tile"), None, None)
    return jax.shard_map(shards, mesh=mesh, in_specs=in_specs, out_specs=out_specs, check_vma=False)
```

time: 18.3 us -> 16.8 us (0.918)
  the two profiles are of different devices: /device:TPU:13 before, /device:TPU:1 now
where the time goes in v2:
time: 16.8 us; the launch traced here: 16.6 us
  Pallas kernels  15.7 us (93%)
  local copies, waits for them, and re-layouts  0.94 us (6%)
    pallas_call x1, Pallas kernels, shards(): pl.pallas_call(functools.partial(kernel, groups, n, per, depth, tile_rows...  15.7 us
    unnamed x1, local copies, waits for them, and re-layouts  0.94 us

profile of v2, /device:TPU:1, one launch (start us, length us, event | category | flops | bytes accessed | tf_op | source)
XLA Modules:
  0.0 16.6 jit_solution(10635861544995577142)
XLA Ops:
  0.0 15.7 %shard_map.55 = bf16[946,4,128]{2,1,0:T(4,128)(2,1)S(1)} custom-call(s32[2,32]{1,0:T(2,128)} %bitcast.5, s32[3,32]{1,0:T(4,128)} %bitcast.4, f32[68]{0:T(128)} %constant.4.clone.rampz_ref, f32[312,128]{1,0:T(8,128)} %constant.5.clone.table_ref, bf16[1,20,256,128]{3,2,1,0:T(8,128)(2,1)} %tile_ref.1), custom_call_target="tpu_custom_call" | custom-call | tf_op jit(solution)/shard_map/pallas_call | solution.py:500
  15.7 0.9 %copy.7 = bf16[4,946,128]{2,0,1:T(4,128)(2,1)} copy(bf16[4,946,128]{2,0,1:T(4,128)(2,1)S(1)} %bitcast.3) | data formatting | bytes 1937408

commit v3 on v2

--- a/solution.py
+++ b/solution.py
@@ -18,8 +18,8 @@
 QUANT = 16
 EDGE = MARGIN + JIT
 PADY = 32
-PADZ = 24
 PIECES = 4
+LOADZ = 4
 
 weight_floor = 0.05
 MESH = pl.DeviceIdType.MESH
@@ -32,11 +32,24 @@
     return np.minimum(rising, rising[::-1])
 
 
+def ramp_at(position, length, ramp_width):
+    inward = jnp.minimum(position, length - 1 - position)
+    t = (inward + 1).astype(jnp.float32) * float(np.pi / 2 / (ramp_width + 1.0))
+    square = t * t
+    sine = jnp.full(t.shape, 1.0 / 6227020800.0, jnp.float32)
+    for term in (-39916800.0, 362880.0, -5040.0, 120.0, -6.0, 1.0):
+        sine = sine * square + 1.0 / term
+    sine = sine * t
+    value = jnp.where(inward < ramp_width, sine * sine, 1.0)
+    return jnp.where(inward < 0, 0.0, value)
+
+
 def round_up(value, step):
     return -(-value // step) * step
 
 
 SOLO = STEPY // 8 * 8
+MAIN = SOLO - 8
 
 
 def pair_start(pair):
@@ -50,13 +63,13 @@
 
 
 def kernel(
-    groups, n, per, depth, tile_rows, shared,
-    offs_ref, fracs_ref, rampz_ref, table_ref, tile_ref, out_ref,
-    head, raw, coef, wa, wb, blend, own_sh, give, got,
+    groups, n, per, depth, tile_rows, shared, trim,
+    offs_ref, fracs_ref, tile_ref, out_ref,
+    lead, head, raw, coef, coef_lead, wa, wb, blend, own_sh, give, got,
     edge_send, far_recv, near_recv, recv, rec,
     offs, fracs, rampz, table,
     small_sem, load_sem, give_sem, got_sem, es_sem, far_sem, near_sem, s_sem, r_sem,
-    above_sem, below_sem,
+    above_sem, below_sem, clear_sem,
 ):
     g = lax.axis_index("slab")
     r = lax.axis_index("tile")
@@ -72,8 +85,8 @@
     frame = SOLO + 2 * shared
     half = SOLO + shared
     rows = out_ref.shape[0]
-    steps = half // 8
-    cut = [steps * i // PIECES * 8 for i in range(PIECES + 1)]
+    steps = MAIN // 8
+    cut = [steps * i // (PIECES - 1) * 8 for i in range(PIECES)] + [half]
     direct = pairs == 2
 
     barrier = pltpu.get_barrier_semaphore()
@@ -88,6 +101,11 @@
     def _():
         pl.semaphore_signal(barrier, inc=1, device_id=(g + 1, r), device_id_type=MESH)
 
+    @pl.when(jnp.logical_and(has_below, high))
+    def _():
+        pl.semaphore_signal(barrier, inc=1, device_id=(g - 1, r), device_id_type=MESH)
+
+    greeted = n - 1 + jnp.where(has_below, 1, 0) + jnp.where(jnp.logical_and(has_above, high), 1, 0)
     far_side = jnp.where(low, 1, 0)
     near_side = 1 - far_side
 
@@ -118,30 +136,38 @@
     def far_owner(i):
         return mirrored(jnp.where(gets_far, far_list[i], far_list[-1 - i]))
 
-    smalls = [
-        pltpu.make_async_copy(source, target, small_sem.at[i])
-        for i, (source, target) in enumerate(
-            [(offs_ref, offs), (fracs_ref, fracs), (rampz_ref, rampz), (table_ref, table)]
-        )
-    ]
-    for small in smalls:
-        small.start()
+    offs_load = pltpu.make_async_copy(offs_ref, offs, small_sem.at[0])
+    fracs_load = pltpu.make_async_copy(fracs_ref, fracs, small_sem.at[1])
     first_owner = far_owner(0)
     head_planes = head.shape[0]
     head_start = jnp.minimum(first_owner * per + MARGIN - JIT, depth - head_planes)
-    head_load = pltpu.make_async_copy(
-        tile_ref.at[0, pl.ds(head_start, head_planes)], head, load_sem.at[0]
-    )
-    head_load.start()
-    load = pltpu.make_async_copy(tile_ref.at[0], raw.at[pl.ds(0, depth)], load_sem.at[1])
-    load.start()
+    lead_rows = lead.shape[1]
+    lead_start = jnp.where(odd, max(2 * shared - (frame - tile_rows), 0) // 8 * 8, 0)
+    head_part = pl.ds(head_start, head_planes)
+    pltpu.make_async_copy(
+        tile_ref.at[0, head_part, pl.ds(pl.multiple_of(lead_start, 8), lead_rows)],
+        lead, load_sem.at[2],
+    ).start()
+    offs_load.start()
+    fracs_load.start()
+    pltpu.make_async_copy(tile_ref.at[0, head_part], head, load_sem.at[0]).start()
+
+    def await_piece(part, sem):
+        pltpu.make_async_copy(part, part, sem).wait()
+
     raw[depth] = jnp.zeros(raw.shape[1:], raw.dtype)
 
+    for at, value in enumerate([0.0, *ramp(depth, 2 * MARGIN), 0.0]):
+        rampz[at] = jnp.float32(value)
+    row = lax.broadcasted_iota(jnp.int32, table.shape, 0) - PADY
+    col = lax.broadcasted_iota(jnp.int32, (8, cols), 1)
+    table[...] = ramp_at(row, tile_rows, RY) * ramp_at(col, cols, RX)[:1]
+
     def rampz_at(z):
-        return rampz[jnp.clip(z + PADZ, 0, rampz.shape[0] - 1)]
-
-    smalls[0].wait()
-    smalls[1].wait()
+        return rampz[jnp.clip(z, -1, depth) + 1]
+
+    offs_load.wait()
+    fracs_load.wait()
     corner = offs[0, me]
     shift = jnp.clip(offs[1, me] - frame_start(r), 0, frame - tile_rows)
     base = g * GROUPZ - corner
@@ -151,29 +177,31 @@
     start_solo = jnp.where(odd, 2 * shared, 0)
     start_own = jnp.where(odd, shared, SOLO)
     start_give = jnp.where(odd, 0, half)
-    parts = [(0, SOLO, start_solo), (SOLO, shared, start_own), (half, shared, start_give)]
-    for at, count, start in parts:
-        row = lax.broadcasted_iota(jnp.int32, (count, tile_rows), 0)
-        col = lax.broadcasted_iota(jnp.int32, (count, tile_rows), 1)
-        behind = col - row + (shift - start)
+    parts = [
+        (0, MAIN, start_solo), (MAIN, shared, start_own),
+        (MAIN + shared, SOLO - MAIN, start_solo + MAIN), (half, shared, start_give),
+    ]
+    def lerps(target, at, count, start, first_col, width):
+        row = lax.broadcasted_iota(jnp.int32, (count, width), 0)
+        col = lax.broadcasted_iota(jnp.int32, (count, width), 1)
+        behind = col - row + (shift - start + first_col)
         lerp_y = jnp.where(behind == 0, 1.0 - fy, jnp.where(behind == 1, fy, 0.0))
-        coef[at : at + count, :tile_rows] = ((1.0 - fz) * lerp_y).astype(jnp.bfloat16)
-        coef[at : at + count, tile_rows:] = (fz * lerp_y).astype(jnp.bfloat16)
-    smalls[2].wait()
-    smalls[3].wait()
-    for at, count, start in parts:
+        target[at : at + count, :width] = ((1.0 - fz) * lerp_y).astype(jnp.bfloat16)
+        target[at : at + count, width:] = (fz * lerp_y).astype(jnp.bfloat16)
+
+    def weights(at, count, start):
         weight = table[pl.ds(PADY + start - shift, count), :]
         lane = lax.broadcasted_iota(jnp.int32, (count, cols), 1)
         wa[at : at + count] = weight * (1.0 - fx)
         wb[at : at + count] = jnp.where(lane < cols - 1, weight * fx, 0.0)
 
-    def planes(store, source, source_start, limit, first, count, lo, hi):
+    def planes(store, source, source_start, limit, factors, first, count, lo, hi):
         at = [jnp.clip(first + j, 0, depth - 1) - source_start for j in range(count)]
         at = [jnp.clip(z, 0, limit) for z in at]
         top = jnp.concatenate([source[z] for z in at], axis=1)
         bottom = jnp.concatenate([source[z + 1] for z in at], axis=1)
         mixed = jnp.dot(
-            coef[lo:hi], jnp.concatenate([top, bottom], axis=0),
+            factors[lo:hi], jnp.concatenate([top, bottom], axis=0),
             preferred_element_type=jnp.float32,
         )
         for j in range(count):
@@ -181,28 +209,32 @@
             value = part * wa[lo:hi] + pltpu.roll(part, cols - 1, 1) * wb[lo:hi]
             store(j, value * rampz_at(first + j))
 
-    def blend_rows(target, at, slot, where_from, first, count, lo, hi):
+    def blend_rows(target, at, start, slot, where_from, first, count, lo, hi):
         def store(j, value):
-            top = min(hi, SOLO)
+            top = min(hi, MAIN)
             if lo < top:
-                target[at, j, lo:top] = value[: top - lo].astype(jnp.bfloat16)
-            if hi > SOLO:
-                own_sh[slot + j] = value[SOLO - lo : half - lo]
+                target[at, start + j, lo:top] = value[: top - lo].astype(jnp.bfloat16)
+            if hi > MAIN:
+                own_sh[slot + j] = value[MAIN - lo : MAIN + shared - lo]
+                target[at, start + j, MAIN + shared : half] = value[
+                    MAIN + shared - lo : half - lo
+                ].astype(jnp.bfloat16)
                 give[slot + j] = value[half - lo :].astype(jnp.bfloat16)
 
         planes(store, *where_from, first, count, lo, hi)
 
-    whole = (raw, 0, depth - 1)
-
-    def blend_owner(owner, lo=0, hi=frame, where_from=whole):
-        blend_rows(blend, owner, owner * per, where_from, base + owner * per, per, lo, hi)
+    whole = (raw, 0, depth - 1, coef)
+
+    def blend_owner(owner, lo=0, hi=frame, where_from=whole, j=0, count=per):
+        first = owner * per + j
+        blend_rows(blend, owner, j, first, where_from, base + first, count, lo, hi)
 
     def edge_slot(side):
         return GROUPZ + side * EDGE
 
     def blend_edge(side):
         first = base + jnp.where(side == 0, GROUPZ, -EDGE)
-        blend_rows(edge_send, side, edge_slot(side), whole, first, EDGE, 0, frame)
+        blend_rows(edge_send, side, 0, edge_slot(side), whole, first, EDGE, 0, frame)
 
     def swap_copy(slot, count, at):
         part = pl.ds(slot, count)
@@ -217,11 +249,11 @@
 
     def join_owner(owner):
         for j in range(per):
-            blend[owner, j, SOLO:half] = joined_rows(owner * per + j)
+            blend[owner, j, MAIN : MAIN + shared] = joined_rows(owner * per + j)
 
     def join_edge(side):
         for p in range(EDGE):
-            edge_send[side, p, SOLO:half] = joined_rows(edge_slot(side) + p)
+            edge_send[side, p, MAIN : MAIN + shared] = joined_rows(edge_slot(side) + p)
 
     def rows_of(i):
         return pl.ds(cut[i], cut[i + 1] - cut[i])
@@ -230,31 +262,41 @@
         away = lax.rem(source_chip - chip + pairs, pairs)
         return jnp.where(away == 0, 0, 1 + (away - 1) * PIECES + i)
 
-    def send(owner, i, when=True):
+    def send(owner, i, when=True, start=0, count=per):
         there = owner // 2
         away = lax.rem(chip - there + pairs, pairs)
         at = jnp.where(away == 0, 0, 1 + (away - 1) * PIECES + i)
-
-        @pl.when(jnp.logical_and(when, owner != r))
-        def _():
-            pltpu.make_async_remote_copy(
-                src_ref=blend.at[owner, :, rows_of(i)], dst_ref=recv.at[r, :, rows_of(i)],
-                send_sem=s_sem, recv_sem=r_sem.at[at],
-                device_id=(g, owner), device_id_type=MESH,
-            ).start()
-
-        @pl.when(jnp.logical_and(when, owner == r))
-        def _():
-            pltpu.make_async_copy(
-                blend.at[owner, :, rows_of(i)], recv.at[r, :, rows_of(i)], r_sem.at[at]
-            ).start()
+        shapes = [(when, 0)] if i < PIECES - 1 else [
+            (jnp.logical_and(when, jnp.logical_not(odd)), 0), (jnp.logical_and(when, odd), trim)
+        ]
+        for condition, less in shapes:
+            part = pl.ds(cut[i], cut[i + 1] - cut[i] - less)
+            source = blend.at[owner, pl.ds(start, count), part]
+            target = recv.at[r, pl.ds(start, count), part]
+
+            @pl.when(jnp.logical_and(condition, owner != r))
+            def _():
+                pltpu.make_async_remote_copy(
+                    src_ref=source, dst_ref=target, send_sem=s_sem, recv_sem=r_sem.at[at],
+                    device_id=(g, owner), device_id_type=MESH,
+                ).start()
+
+            @pl.when(jnp.logical_and(condition, owner == r))
+            def _():
+                pltpu.make_async_copy(source, target, r_sem.at[at]).start()
+
+    def inner(o):
+        taking = sum(o * per + j >= GROUPZ - EDGE for j in range(per))
+        free_count = per - taking
+        return jnp.where(low, 0, taking), free_count, jnp.where(low, free_count, 0), taking
 
     def await_far(source_chip, i):
-        part = recv.at[pl.ds(2 * source_chip, 2), :, rows_of(i)]
+        less = trim // 2 if i == PIECES - 1 else 0
+        part = recv.at[pl.ds(2 * source_chip, 2), :, pl.ds(cut[i], cut[i + 1] - cut[i] - less)]
         pltpu.make_async_copy(part, part, r_sem.at[came(source_chip, i)]).wait()
 
     def await_own():
-        part = recv.at[pl.ds(2 * chip, 2)]
+        part = recv.at[pl.ds(2 * chip, 2), :, pl.ds(0, half - trim // 2)]
         pltpu.make_async_copy(part, part, r_sem.at[0]).wait()
 
     def send_far(i):
@@ -278,9 +320,6 @@
                 send_sem=es_sem.at[1], recv_sem=near_sem.at[i],
                 device_id=(g + 1 - 2 * near_side, near_target), device_id_type=MESH,
             ).start()
-
-    def await_piece(part, sem):
-        pltpu.make_async_copy(part, part, sem).wait()
 
     def add_edge(side, source, i):
         for p in range(EDGE):
@@ -291,53 +330,64 @@
                 blend[owner, j, a:b].astype(jnp.float32) + source[p, a:b].astype(jnp.float32)
             ).astype(jnp.bfloat16)
 
-    near_head = (head, head_start, head_planes - 2)
-    head_load.wait()
-    blend_owner(first_owner, 0, cut[1], near_head)
-    pl.semaphore_wait(barrier, n - 1 + jnp.where(has_below, 1, 0))
+    lerps(coef_lead, 0, cut[1], start_solo, lead_start, lead_rows)
+    weights(0, cut[1], start_solo)
+    await_piece(lead, load_sem.at[2])
+    for z in range(0, depth, LOADZ):
+        part = pl.ds(z, min(LOADZ, depth - z))
+        pltpu.make_async_copy(tile_ref.at[0, part], raw.at[part], load_sem.at[1]).start()
     not_far = jnp.logical_not(gets_far)
-    send(first_owner, 0, True if far_free else not_far)
-
-    @pl.when(has_below)
+    first_when = True if far_free else not_far
+    blend_owner(first_owner, 0, cut[1], (lead, head_start, head_planes - 2, coef_lead))
+    pl.semaphore_wait(barrier, greeted)
+    send(first_owner, 0, first_when)
+
+    @pl.when(jnp.logical_and(has_below, low))
     def _():
         pl.semaphore_signal(above_sem, inc=1, device_id=(g - 1, r), device_id_type=MESH)
 
-    blend_owner(first_owner, cut[1], frame, near_head)
+    if direct:
+        @pl.when(jnp.logical_and(has_above, high))
+        def _():
+            pl.semaphore_signal(below_sem, inc=1, device_id=(g + 1, r), device_id_type=MESH)
+
+    for at, count, start in parts:
+        lerps(coef, at, count, start, 0, tile_rows)
+    weights(cut[1], MAIN - cut[1], start_solo + cut[1])
+    for at, count, start in parts[1:]:
+        weights(at, count, start)
+    await_piece(head, load_sem.at[0])
+    blend_owner(first_owner, cut[1], frame, (head, head_start, head_planes - 2, coef))
     for i in range(1, PIECES - 1):
-        send(first_owner, i, True if far_free else not_far)
+        send(first_owner, i, first_when)
     swap_copy(first_owner * per, per, 0).start()
 
-    load.wait()
+    await_piece(raw.at[pl.ds(0, depth)], load_sem.at[1])
     blend_edge(far_side)
     swap_copy(edge_slot(far_side), EDGE, 0).start()
-
-    @pl.when(low)
-    def _():
-        for i in range(PIECES - 1):
-            send_far(i)
+    for i in range(PIECES - 1):
+        send_far(i)
 
     for at in range(1, len(far_list)):
         owner = far_owner(at)
         blend_owner(owner)
         swap_copy(owner * per, per, 1).start()
 
-    @pl.when(jnp.logical_and(has_above, high))
-    def _():
-        pl.semaphore_wait(above_sem, 1)
-        if direct:
-            pl.semaphore_signal(below_sem, inc=1, device_id=(g + 1, r), device_id_type=MESH)
-        for i in range(PIECES - 1):
-            send_far(i)
-
     await_piece(got.at[pl.ds(0, per + EDGE)], got_sem.at[0])
     join_owner(first_owner)
-    send(first_owner, PIECES - 1, True if far_free else not_far)
+    send(first_owner, PIECES - 1, first_when)
     join_edge(far_side)
     send_far(PIECES - 1)
     for at in range(1, len(far_list)):
         owner = far_owner(at)
         for i in range(PIECES - 1):
-            send(owner, i, True if at < len(far_free) else not_far)
+            if at < len(far_free):
+                send(owner, i)
+            else:
+                send(owner, i, not_far)
+                start, count, _, _ = inner(far_list[at])
+                if count:
+                    send(owner, i, gets_far, start, count)
 
     for o in near_list:
         owner = mirrored(o)
@@ -349,18 +399,6 @@
         @pl.when(jnp.logical_not(takes_near))
         def _():
             near_recv[...] = jnp.zeros_like(near_recv)
-
-    await_piece(got.at[pl.ds(0, GROUPZ - per + EDGE)], got_sem.at[1])
-    for at in range(1, len(far_list)):
-        owner = far_owner(at)
-        join_owner(owner)
-        send(owner, PIECES - 1, True if at < len(far_free) else not_far)
-    for o in near_list:
-        owner = mirrored(o)
-        join_owner(owner)
-        for i in range(PIECES):
-            send(owner, i, True if direct or o in near_free else jnp.logical_not(gets_near))
-    join_edge(near_side)
 
     rec[...] = jnp.zeros_like(rec)
     for k in range(n):
@@ -379,6 +417,24 @@
             rec[j, s : s + frame] = rec[j, s : s + frame] + totals[j]
     rec[...] = 1.0 / jnp.maximum(rec[...], weight_floor)
 
+    await_piece(got.at[pl.ds(0, GROUPZ - per + EDGE)], got_sem.at[1])
+    for at in range(1, len(far_list)):
+        owner = far_owner(at)
+        join_owner(owner)
+        if at < len(far_free):
+            send(owner, PIECES - 1)
+        else:
+            send(owner, PIECES - 1, not_far)
+            start, count, _, _ = inner(far_list[at])
+            if count:
+                send(owner, PIECES - 1, gets_far, start, count)
+    for o in near_list:
+        owner = mirrored(o)
+        join_owner(owner)
+        for i in range(PIECES):
+            send(owner, i, True if direct or o in near_free else jnp.logical_not(gets_near))
+    join_edge(near_side)
+
     @pl.when(jnp.logical_and(has_above, low))
     def _():
         pl.semaphore_wait(above_sem, 1)
@@ -394,7 +450,17 @@
             await_piece(far_recv.at[:, rows_of(i)], far_sem.at[i])
             add_edge(far_side, far_recv, i)
             for o in far_bound:
-                send(mirrored(o), i)
+                _, _, start, count = inner(o)
+                send(mirrored(o), i, True, start, count)
+
+        if i == 0:
+            @pl.when(sends_to(far_side))
+            def _():
+                await_piece(far_recv, es_sem.at[0])
+                pl.semaphore_signal(
+                    clear_sem, inc=1, device_id=(g, partner), device_id_type=MESH
+                )
+                pl.semaphore_wait(clear_sem, 1)
 
         send_near(i)
 
@@ -410,12 +476,13 @@
     def spans(k, i):
         solo_at = pair_start(k // 2) + (k % 2) * (SOLO + 2 * shared)
         shared_at = pair_start(k // 2) + SOLO + (k % 2) * shared
-        a, b = cut[i], cut[i + 1]
-        found = [(solo_at + a, solo_at + min(b, SOLO), solo_at)] if a < SOLO else []
-        if b > SOLO:
-            a = max(a, SOLO)
-            found.append((shared_at + a - SOLO, shared_at + b - SOLO, shared_at - SOLO))
-        return found
+        if i < PIECES - 1:
+            return [(solo_at + cut[i], solo_at + cut[i + 1], solo_at)]
+        end = solo_at + SOLO - (k % 2) * trim
+        return [
+            (shared_at, shared_at + shared, shared_at - MAIN),
+            (solo_at + MAIN, end, solo_at - shared),
+        ]
 
     segments = [(k, i, *span) for k in range(n) for i in range(PIECES) for span in spans(k, i)]
     marks = sorted({min(end, rows) for item in segments for end in item[2:4]})
@@ -464,15 +531,15 @@
         for item in intervals:
             finish(*item)
 
-    def await_sent(part, sem):
-        pltpu.make_async_copy(part, part, sem).wait()
-
-    await_sent(give, give_sem)
-    await_sent(blend.at[pl.ds(0, n - 1)], s_sem)
-    for at, side in enumerate((far_side, near_side)):
-        @pl.when(sends_to(side))
-        def _():
-            await_sent(far_recv, es_sem.at[at])
+    await_piece(give, give_sem)
+    for is_odd in (False, True):
+        @pl.when(odd == is_odd)
+        def _():
+            await_piece(blend.at[pl.ds(0, n - 1), :, pl.ds(0, half - is_odd * trim)], s_sem)
+
+    @pl.when(sends_to(near_side))
+    def _():
+        await_piece(far_recv, es_sem.at[1])
 
 
 def solution(mesh):
@@ -487,25 +554,24 @@
         )
         shared = round_up(max(reach - SOLO, 16), 16) // 2
         frame, half = SOLO + 2 * shared, SOLO + shared
+        trim = min(frame - reach, SOLO - MAIN - 4) // 4 * 4
         acc_rows = round_up(max(rows, frame_start(n - 1) + frame), 16)
         head = per + 2 * JIT + 1
-        plane = ramp(tile_rows, RY)[:, None] * ramp(cols, RX)[None, :]
-        table = np.zeros((round_up(PADY + frame + 8, 8), cols), np.float32)
-        table[PADY : PADY + tile_rows] = plane
-        rampz = np.zeros((depth + 2 * PADZ,), np.float32)
-        rampz[PADZ : PADZ + depth] = ramp(depth, 2 * MARGIN)
+        lead = round_up(MAIN // (PIECES - 1) + frame - tile_rows + 8, 16)
         bf16, f32 = jnp.bfloat16, jnp.float32
         dma, signal = pltpu.SemaphoreType.DMA, pltpu.SemaphoreType.REGULAR
         slots = GROUPZ + 2 * EDGE
         joined = pl.pallas_call(
-            functools.partial(kernel, groups, n, per, depth, tile_rows, shared),
+            functools.partial(kernel, groups, n, per, depth, tile_rows, shared, trim),
             out_shape=pltpu.VMEM((rows, per, cols), bf16),
-            in_specs=[pl.BlockSpec(memory_space=pl.ANY)] * 5,
+            in_specs=[pl.BlockSpec(memory_space=pl.ANY)] * 3,
             out_specs=pl.BlockSpec(memory_space=pltpu.VMEM),
             scratch_shapes=[
+                pltpu.VMEM((head, lead, cols), bf16),
                 pltpu.VMEM((head, tile_rows, cols), bf16),
                 pltpu.VMEM((depth + 1, tile_rows, cols), bf16),
                 pltpu.VMEM((frame, 2 * tile_rows), bf16),
+                pltpu.VMEM((SOLO, 2 * lead), bf16),
                 pltpu.VMEM((frame, cols), f32),
                 pltpu.VMEM((frame, cols), f32),
                 pltpu.VMEM((n, per, half, cols), bf16),
@@ -519,14 +585,14 @@
                 pltpu.VMEM((per, acc_rows, cols), f32),
                 pltpu.SMEM((offsets.shape[1], offsets.shape[0]), jnp.int32),
                 pltpu.SMEM((fracs.shape[1], fracs.shape[0]), jnp.int32),
-                pltpu.SMEM(rampz.shape, f32),
-                pltpu.VMEM(table.shape, f32),
-                dma((4,)), dma((2,)), dma, dma((2,)), dma((2,)),
+                pltpu.SMEM((depth + 2,), f32),
+                pltpu.VMEM((round_up(PADY + frame + 8, 8), cols), f32),
+                dma((2,)), dma((3,)), dma, dma((2,)), dma((2,)),
                 dma((PIECES,)), dma((PIECES,)), dma, dma(((n // 2 - 1) * PIECES + 1,)),
-                signal, signal,
+                signal, signal, signal,
             ],
             compiler_params=pltpu.CompilerParams(collective_id=0, has_side_effects=True),
-        )(offsets.T, fracs.T, jnp.asarray(rampz), jnp.asarray(table), tiles)
+        )(offsets.T, fracs.T, tiles)
         return jnp.transpose(joined, (1, 0, 2))
 
     in_specs = (P(("slab", "tile"), None, None, None), P(), P())

time: 16.8 us -> 16.4 us (0.976)
  Pallas kernels: 15.7 us -> 15.3 us
    pallas_call x1, Pallas kernels: 15.7 us -> 15.3 us  [shards(): pl.pallas_call(functools.partial(kernel, groups, n, per, depth, tile_rows...]
where the time goes in v3:
time: 16.4 us; the launch traced here: 16.3 us
  Pallas kernels  15.3 us (93%)
  local copies, waits for them, and re-layouts  0.94 us (6%)
    pallas_call x1, Pallas kernels, shards(): pl.pallas_call(functools.partial(kernel, groups, n, per, depth, tile_rows...  15.3 us
    unnamed x1, local copies, waits for them, and re-layouts  0.94 us

profile of v3, /device:TPU:1, one launch (start us, length us, event | category | flops | bytes accessed | tf_op | source)
XLA Modules:
  0.0 16.3 jit_solution(10033246020367110736)
XLA Ops:
  0.0 15.3 %shard_map.37 = bf16[946,4,128]{2,1,0:T(4,128)(2,1)S(1)} custom-call(s32[2,32]{1,0:T(2,128)} %bitcast.5, s32[3,32]{1,0:T(4,128)} %bitcast.4, bf16[1,20,256,128]{3,2,1,0:T(8,128)(2,1)} %tile_ref.1), custom_call_target="tpu_custom_call" | custom-call | tf_op jit(solution)/shard_map/pallas_call | solution.py:564
  15.3 0.9 %copy.5 = bf16[4,946,128]{2,0,1:T(4,128)(2,1)} copy(bf16[4,946,128]{2,0,1:T(4,128)(2,1)S(1)} %bitcast.3) | data formatting | bytes 1937408

commit v4 on v3

--- a/solution.py
+++ b/solution.py
@@ -18,7 +18,7 @@
 QUANT = 16
 EDGE = MARGIN + JIT
 PADY = 32
-PIECES = 4
+PIECES = 3
 LOADZ = 4
 
 weight_floor = 0.05
@@ -50,6 +50,8 @@
 
 SOLO = STEPY // 8 * 8
 MAIN = SOLO - 8
+FIRST = MAIN // 24 * 8
+DETOUR = 32
 
 
 def pair_start(pair):
@@ -63,12 +65,12 @@
 
 
 def kernel(
-    groups, n, per, depth, tile_rows, shared, trim,
+    groups, n, per, depth, tile_rows, shared, trim, stride,
     offs_ref, fracs_ref, tile_ref, out_ref,
     lead, head, raw, coef, coef_lead, wa, wb, blend, own_sh, give, got,
-    edge_send, far_recv, near_recv, recv, rec,
+    edge_send, far_recv, near_recv, recv, relay, rec,
     offs, fracs, rampz, table,
-    small_sem, load_sem, give_sem, got_sem, es_sem, far_sem, near_sem, s_sem, r_sem,
+    small_sem, load_sem, give_sem, got_sem, es_sem, far_sem, near_sem, s_sem, r_sem, relay_sem,
     above_sem, below_sem, clear_sem,
 ):
     g = lax.axis_index("slab")
@@ -85,8 +87,7 @@
     frame = SOLO + 2 * shared
     half = SOLO + shared
     rows = out_ref.shape[0]
-    steps = MAIN // 8
-    cut = [steps * i // (PIECES - 1) * 8 for i in range(PIECES)] + [half]
+    cut = [0, FIRST, MAIN, half]
     direct = pairs == 2
 
     barrier = pltpu.get_barrier_semaphore()
@@ -105,7 +106,17 @@
     def _():
         pl.semaphore_signal(barrier, inc=1, device_id=(g - 1, r), device_id_type=MESH)
 
+    detour = direct and groups > stride
+    relays = jnp.logical_and(g == stride, odd)
+    source = jnp.logical_and(g == 0, jnp.logical_and(high, odd)) if detour else False
+    if detour:
+        @pl.when(jnp.logical_and(relays, high))
+        def _():
+            pl.semaphore_signal(barrier, inc=1, device_id=(0, r), device_id_type=MESH)
+
     greeted = n - 1 + jnp.where(has_below, 1, 0) + jnp.where(jnp.logical_and(has_above, high), 1, 0)
+    if detour:
+        greeted = greeted + jnp.where(source, 1, 0)
     far_side = jnp.where(low, 1, 0)
     near_side = 1 - far_side
 
@@ -262,28 +273,28 @@
         away = lax.rem(source_chip - chip + pairs, pairs)
         return jnp.where(away == 0, 0, 1 + (away - 1) * PIECES + i)
 
-    def send(owner, i, when=True, start=0, count=per):
+    def send(owner, i, when=True, start=0, count=per, less=0):
         there = owner // 2
         away = lax.rem(chip - there + pairs, pairs)
         at = jnp.where(away == 0, 0, 1 + (away - 1) * PIECES + i)
-        shapes = [(when, 0)] if i < PIECES - 1 else [
+        shapes = [(when, less)] if i < PIECES - 1 else [
             (jnp.logical_and(when, jnp.logical_not(odd)), 0), (jnp.logical_and(when, odd), trim)
         ]
-        for condition, less in shapes:
-            part = pl.ds(cut[i], cut[i + 1] - cut[i] - less)
-            source = blend.at[owner, pl.ds(start, count), part]
+        for condition, fewer in shapes:
+            part = pl.ds(cut[i], cut[i + 1] - cut[i] - fewer)
+            held = blend.at[owner, pl.ds(start, count), part]
             target = recv.at[r, pl.ds(start, count), part]
 
             @pl.when(jnp.logical_and(condition, owner != r))
             def _():
                 pltpu.make_async_remote_copy(
-                    src_ref=source, dst_ref=target, send_sem=s_sem, recv_sem=r_sem.at[at],
+                    src_ref=held, dst_ref=target, send_sem=s_sem, recv_sem=r_sem.at[at],
                     device_id=(g, owner), device_id_type=MESH,
                 ).start()
 
             @pl.when(jnp.logical_and(condition, owner == r))
             def _():
-                pltpu.make_async_copy(source, target, r_sem.at[at]).start()
+                pltpu.make_async_copy(held, target, r_sem.at[at]).start()
 
     def inner(o):
         taking = sum(o * per + j >= GROUPZ - EDGE for j in range(per))
@@ -358,8 +369,20 @@
         weights(at, count, start)
     await_piece(head, load_sem.at[0])
     blend_owner(first_owner, cut[1], frame, (head, head_start, head_planes - 2, coef))
-    for i in range(1, PIECES - 1):
-        send(first_owner, i, first_when)
+    if detour:
+        @pl.when(source)
+        def _():
+            pltpu.make_async_remote_copy(
+                src_ref=blend.at[first_owner, :, pl.ds(MAIN - DETOUR, DETOUR)], dst_ref=relay,
+                send_sem=s_sem, recv_sem=relay_sem.at[0],
+                device_id=(stride, r), device_id_type=MESH,
+            ).start()
+
+        send(first_owner, 1, source, less=DETOUR)
+        send(first_owner, 1, jnp.logical_not(source))
+    else:
+        for i in range(1, PIECES - 1):
+            send(first_owner, i, first_when)
     swap_copy(first_owner * per, per, 0).start()
 
     await_piece(raw.at[pl.ds(0, depth)], load_sem.at[1])
@@ -399,6 +422,15 @@
         @pl.when(jnp.logical_not(takes_near))
         def _():
             near_recv[...] = jnp.zeros_like(near_recv)
+
+    if detour:
+        @pl.when(jnp.logical_and(relays, high))
+        def _():
+            await_piece(relay, relay_sem.at[0])
+            pltpu.make_async_remote_copy(
+                src_ref=relay, dst_ref=relay, send_sem=relay_sem.at[1], recv_sem=relay_sem.at[0],
+                device_id=(g, r - n // 2), device_id_type=MESH,
+            ).start()
 
     rec[...] = jnp.zeros_like(rec)
     for k in range(n):
@@ -473,6 +505,16 @@
                 for o in near_bound:
                     send(mirrored(o), i)
 
+    if detour:
+        @pl.when(jnp.logical_and(relays, low))
+        def _():
+            await_piece(relay, relay_sem.at[0])
+            pltpu.make_async_remote_copy(
+                src_ref=relay, dst_ref=recv.at[r + n // 2, :, pl.ds(MAIN - DETOUR, DETOUR)],
+                send_sem=relay_sem.at[1], recv_sem=r_sem.at[2],
+                device_id=(0, 0), device_id_type=MESH,
+            ).start()
+
     def spans(k, i):
         solo_at = pair_start(k // 2) + (k % 2) * (SOLO + 2 * shared)
         shared_at = pair_start(k // 2) + SOLO + (k % 2) * shared
@@ -531,6 +573,11 @@
         for item in intervals:
             finish(*item)
 
+    if detour:
+        @pl.when(relays)
+        def _():
+            await_piece(relay, relay_sem.at[1])
+
     await_piece(give, give_sem)
     for is_odd in (False, True):
         @pl.when(odd == is_odd)
@@ -544,6 +591,7 @@
 
 def solution(mesh):
     groups, n = mesh.shape["slab"], mesh.shape["tile"]
+    stride = len({getattr(d, "coords", (i % 2,))[0] for i, d in enumerate(mesh.devices.flat)})
 
     def shards(tiles, offsets, fracs):
         _, depth, tile_rows, cols = tiles.shape
@@ -557,12 +605,14 @@
         trim = min(frame - reach, SOLO - MAIN - 4) // 4 * 4
         acc_rows = round_up(max(rows, frame_start(n - 1) + frame), 16)
         head = per + 2 * JIT + 1
-        lead = round_up(MAIN // (PIECES - 1) + frame - tile_rows + 8, 16)
+        lead = round_up(FIRST + frame - tile_rows + 8, 16)
         bf16, f32 = jnp.bfloat16, jnp.float32
         dma, signal = pltpu.SemaphoreType.DMA, pltpu.SemaphoreType.REGULAR
         slots = GROUPZ + 2 * EDGE
         joined = pl.pallas_call(
-            functools.partial(kernel, groups, n, per, depth, tile_rows, shared, trim),
+            functools.partial(
+                kernel, groups, n, per, depth, tile_rows, shared, trim, stride
+            ),
             out_shape=pltpu.VMEM((rows, per, cols), bf16),
             in_specs=[pl.BlockSpec(memory_space=pl.ANY)] * 3,
             out_specs=pl.BlockSpec(memory_space=pltpu.VMEM),
@@ -582,13 +632,14 @@
                 pltpu.VMEM((EDGE, half, cols), bf16),
                 pltpu.VMEM((2, EDGE, half, cols), bf16),
                 pltpu.VMEM((n, per, half, cols), bf16),
+                pltpu.VMEM((per, DETOUR, cols), bf16),
                 pltpu.VMEM((per, acc_rows, cols), f32),
                 pltpu.SMEM((offsets.shape[1], offsets.shape[0]), jnp.int32),
                 pltpu.SMEM((fracs.shape[1], fracs.shape[0]), jnp.int32),
                 pltpu.SMEM((depth + 2,), f32),
                 pltpu.VMEM((round_up(PADY + frame + 8, 8), cols), f32),
                 dma((2,)), dma((3,)), dma, dma((2,)), dma((2,)),
-                dma((PIECES,)), dma((PIECES,)), dma, dma(((n // 2 - 1) * PIECES + 1,)),
+                dma((PIECES,)), dma((PIECES,)), dma, dma(((n // 2 - 1) * PIECES + 1,)), dma((2,)),
                 signal, signal, signal,
             ],
             compiler_params=pltpu.CompilerParams(collective_id=0, has_side_effects=True),

time: 16.4 us -> 16.1 us (0.982)
  Pallas kernels: 15.3 us -> 15 us
    pallas_call x1, Pallas kernels: 15.3 us -> 15 us  [shards(): pl.pallas_call(functools.partial(kernel, groups, n, per, depth, tile_rows...]
where the time goes in v4:
time: 16.1 us; the launch traced here: 16 us
  Pallas kernels  15 us (93%)
  local copies, waits for them, and re-layouts  0.94 us (6%)
    pallas_call x1, Pallas kernels, shards(): pl.pallas_call(functools.partial(kernel, groups, n, per, depth, tile_rows...  15 us
    unnamed x1, local copies, waits for them, and re-layouts  0.94 us

profile of v4, /device:TPU:1, one launch (start us, length us, event | category | flops | bytes accessed | tf_op | source)
XLA Modules:
  0.0 16.0 jit_solution(3758628986761488360)
XLA Ops:
  0.0 15.0 %shard_map.37 = bf16[946,4,128]{2,1,0:T(4,128)(2,1)S(1)} custom-call(s32[2,32]{1,0:T(2,128)} %bitcast.5, s32[3,32]{1,0:T(4,128)} %bitcast.4, bf16[1,20,256,128]{3,2,1,0:T(8,128)(2,1)} %tile_ref.1), custom_call_target="tpu_custom_call" | custom-call | tf_op jit(solution)/shard_map/pallas_call | solution.py:612
  15.0 0.9 %copy.5 = bf16[4,946,128]{2,0,1:T(4,128)(2,1)} copy(bf16[4,946,128]{2,0,1:T(4,128)(2,1)S(1)} %bitcast.3) | data formatting | bytes 1937408

commit v5 on v4

--- a/solution.py
+++ b/solution.py
@@ -19,7 +19,6 @@
 EDGE = MARGIN + JIT
 PADY = 32
 PIECES = 3
-LOADZ = 4
 
 weight_floor = 0.05
 MESH = pl.DeviceIdType.MESH
@@ -51,7 +50,7 @@
 SOLO = STEPY // 8 * 8
 MAIN = SOLO - 8
 FIRST = MAIN // 24 * 8
-DETOUR = 32
+DETOUR = 40
 
 
 def pair_start(pair):
@@ -67,7 +66,7 @@
 def kernel(
     groups, n, per, depth, tile_rows, shared, trim, stride,
     offs_ref, fracs_ref, tile_ref, out_ref,
-    lead, head, raw, coef, coef_lead, wa, wb, blend, own_sh, give, got,
+    lead, raw, coef, coef_lead, wa, wb, blend, own_sh, give, got,
     edge_send, far_recv, near_recv, recv, relay, rec,
     offs, fracs, rampz, table,
     small_sem, load_sem, give_sem, got_sem, es_sem, far_sem, near_sem, s_sem, r_sem, relay_sem,
@@ -108,11 +107,12 @@
 
     detour = direct and groups > stride
     relays = jnp.logical_and(g == stride, odd)
-    source = jnp.logical_and(g == 0, jnp.logical_and(high, odd)) if detour else False
+    source_rank = n // 2
+    source = jnp.logical_and(g == 0, r == source_rank) if detour else False
     if detour:
         @pl.when(jnp.logical_and(relays, high))
         def _():
-            pl.semaphore_signal(barrier, inc=1, device_id=(0, r), device_id_type=MESH)
+            pl.semaphore_signal(barrier, inc=1, device_id=(0, source_rank), device_id_type=MESH)
 
     greeted = n - 1 + jnp.where(has_below, 1, 0) + jnp.where(jnp.logical_and(has_above, high), 1, 0)
     if detour:
@@ -150,18 +150,18 @@
     offs_load = pltpu.make_async_copy(offs_ref, offs, small_sem.at[0])
     fracs_load = pltpu.make_async_copy(fracs_ref, fracs, small_sem.at[1])
     first_owner = far_owner(0)
-    head_planes = head.shape[0]
+    head_planes = lead.shape[0]
     head_start = jnp.minimum(first_owner * per + MARGIN - JIT, depth - head_planes)
     lead_rows = lead.shape[1]
     lead_start = jnp.where(odd, max(2 * shared - (frame - tile_rows), 0) // 8 * 8, 0)
     head_part = pl.ds(head_start, head_planes)
     pltpu.make_async_copy(
         tile_ref.at[0, head_part, pl.ds(pl.multiple_of(lead_start, 8), lead_rows)],
-        lead, load_sem.at[2],
+        lead, load_sem.at[0],
     ).start()
     offs_load.start()
     fracs_load.start()
-    pltpu.make_async_copy(tile_ref.at[0, head_part], head, load_sem.at[0]).start()
+    pltpu.make_async_copy(tile_ref.at[0], raw.at[pl.ds(0, depth)], load_sem.at[1]).start()
 
     def await_piece(part, sem):
         pltpu.make_async_copy(part, part, sem).wait()
@@ -343,12 +343,10 @@
 
     lerps(coef_lead, 0, cut[1], start_solo, lead_start, lead_rows)
     weights(0, cut[1], start_solo)
-    await_piece(lead, load_sem.at[2])
-    for z in range(0, depth, LOADZ):
-        part = pl.ds(z, min(LOADZ, depth - z))
-        pltpu.make_async_copy(tile_ref.at[0, part], raw.at[part], load_sem.at[1]).start()
+    await_piece(lead, load_sem.at[0])
     not_far = jnp.logical_not(gets_far)
     first_when = True if far_free else not_far
+    held_back = jnp.logical_and(jnp.logical_and(high, odd), gets_far) if direct else False
     blend_owner(first_owner, 0, cut[1], (lead, head_start, head_planes - 2, coef_lead))
     pl.semaphore_wait(barrier, greeted)
     send(first_owner, 0, first_when)
@@ -367,15 +365,15 @@
     weights(cut[1], MAIN - cut[1], start_solo + cut[1])
     for at, count, start in parts[1:]:
         weights(at, count, start)
-    await_piece(head, load_sem.at[0])
-    blend_owner(first_owner, cut[1], frame, (head, head_start, head_planes - 2, coef))
+    await_piece(raw.at[pl.ds(0, depth)], load_sem.at[1])
+    blend_owner(first_owner, cut[1], frame)
     if detour:
         @pl.when(source)
         def _():
             pltpu.make_async_remote_copy(
                 src_ref=blend.at[first_owner, :, pl.ds(MAIN - DETOUR, DETOUR)], dst_ref=relay,
                 send_sem=s_sem, recv_sem=relay_sem.at[0],
-                device_id=(stride, r), device_id_type=MESH,
+                device_id=(stride, source_rank + 1), device_id_type=MESH,
             ).start()
 
         send(first_owner, 1, source, less=DETOUR)
@@ -385,7 +383,6 @@
             send(first_owner, i, first_when)
     swap_copy(first_owner * per, per, 0).start()
 
-    await_piece(raw.at[pl.ds(0, depth)], load_sem.at[1])
     blend_edge(far_side)
     swap_copy(edge_slot(far_side), EDGE, 0).start()
     for i in range(PIECES - 1):
@@ -398,7 +395,7 @@
 
     await_piece(got.at[pl.ds(0, per + EDGE)], got_sem.at[0])
     join_owner(first_owner)
-    send(first_owner, PIECES - 1, first_when)
+    send(first_owner, PIECES - 1, jnp.logical_and(first_when, jnp.logical_not(held_back)))
     join_edge(far_side)
     send_far(PIECES - 1)
     for at in range(1, len(far_list)):
@@ -496,7 +493,9 @@
 
         send_near(i)
 
-    if not direct:
+    if direct:
+        send(first_owner, PIECES - 1, held_back)
+    else:
         @pl.when(gets_near)
         def _():
             for i in range(PIECES):
@@ -510,7 +509,7 @@
         def _():
             await_piece(relay, relay_sem.at[0])
             pltpu.make_async_remote_copy(
-                src_ref=relay, dst_ref=recv.at[r + n // 2, :, pl.ds(MAIN - DETOUR, DETOUR)],
+                src_ref=relay, dst_ref=recv.at[source_rank, :, pl.ds(MAIN - DETOUR, DETOUR)],
                 send_sem=relay_sem.at[1], recv_sem=r_sem.at[2],
                 device_id=(0, 0), device_id_type=MESH,
             ).start()
@@ -618,7 +617,6 @@
             out_specs=pl.BlockSpec(memory_space=pltpu.VMEM),
             scratch_shapes=[
                 pltpu.VMEM((head, lead, cols), bf16),
-                pltpu.VMEM((head, tile_rows, cols), bf16),
                 pltpu.VMEM((depth + 1, tile_rows, cols), bf16),
                 pltpu.VMEM((frame, 2 * tile_rows), bf16),
                 pltpu.VMEM((SOLO, 2 * lead), bf16),
@@ -638,7 +636,7 @@
                 pltpu.SMEM((fracs.shape[1], fracs.shape[0]), jnp.int32),
                 pltpu.SMEM((depth + 2,), f32),
                 pltpu.VMEM((round_up(PADY + frame + 8, 8), cols), f32),
-                dma((2,)), dma((3,)), dma, dma((2,)), dma((2,)),
+                dma((2,)), dma((2,)), dma, dma((2,)), dma((2,)),
                 dma((PIECES,)), dma((PIECES,)), dma, dma(((n // 2 - 1) * PIECES + 1,)), dma((2,)),
                 signal, signal, signal,
             ],

time: 16.1 us -> 16.1 us (level); the launches traced: 16 us -> 15.8 us
    pallas_call x1, Pallas kernels: 15 us -> 14.9 us  [shards(): pl.pallas_call(functools.partial(kernel, groups, n, per, depth, tile_rows...]
where the time goes in v5:
time: 16.1 us; the launch traced here: 15.8 us
  Pallas kernels  14.9 us (93%)
  local copies, waits for them, and re-layouts  0.94 us (6%)
    pallas_call x1, Pallas kernels, shards(): pl.pallas_call(functools.partial(kernel, groups, n, per, depth, tile_rows...  14.9 us
    unnamed x1, local copies, waits for them, and re-layouts  0.94 us

profile of v5, /device:TPU:1, one launch (start us, length us, event | category | flops | bytes accessed | tf_op | source)
XLA Modules:
  0.0 15.8 jit_solution(11712935557431566277)
XLA Ops:
  0.0 14.9 %shard_map.37 = bf16[946,4,128]{2,1,0:T(4,128)(2,1)S(1)} custom-call(s32[2,32]{1,0:T(2,128)} %bitcast.5, s32[3,32]{1,0:T(4,128)} %bitcast.4, bf16[1,20,256,128]{3,2,1,0:T(8,128)(2,1)} %tile_ref.1), custom_call_target="tpu_custom_call" | custom-call | tf_op jit(solution)/shard_map/pallas_call | solution.py:611
  14.9 0.9 %copy.5 = bf16[4,946,128]{2,0,1:T(4,128)(2,1)} copy(bf16[4,946,128]{2,0,1:T(4,128)(2,1)S(1)} %bitcast.3) | data formatting | bytes 1937408

commit v6 on v5

--- a/solution.py
+++ b/solution.py
@@ -50,7 +50,7 @@
 SOLO = STEPY // 8 * 8
 MAIN = SOLO - 8
 FIRST = MAIN // 24 * 8
-DETOUR = 40
+DETOUR = 24
 
 
 def pair_start(pair):
@@ -105,8 +105,9 @@
     def _():
         pl.semaphore_signal(barrier, inc=1, device_id=(g - 1, r), device_id_type=MESH)
 
+    routes = sorted({stride, 1}, reverse=True)
     detour = direct and groups > stride
-    relays = jnp.logical_and(g == stride, odd)
+    relays = jnp.logical_and(functools.reduce(jnp.logical_or, [g == at for at in routes]), odd)
     source_rank = n // 2
     source = jnp.logical_and(g == 0, r == source_rank) if detour else False
     if detour:
@@ -116,7 +117,7 @@
 
     greeted = n - 1 + jnp.where(has_below, 1, 0) + jnp.where(jnp.logical_and(has_above, high), 1, 0)
     if detour:
-        greeted = greeted + jnp.where(source, 1, 0)
+        greeted = greeted + jnp.where(source, len(routes), 0)
     far_side = jnp.where(low, 1, 0)
     near_side = 1 - far_side
 
@@ -370,13 +371,15 @@
     if detour:
         @pl.when(source)
         def _():
-            pltpu.make_async_remote_copy(
-                src_ref=blend.at[first_owner, :, pl.ds(MAIN - DETOUR, DETOUR)], dst_ref=relay,
-                send_sem=s_sem, recv_sem=relay_sem.at[0],
-                device_id=(stride, source_rank + 1), device_id_type=MESH,
-            ).start()
-
-        send(first_owner, 1, source, less=DETOUR)
+            for i, at in enumerate(routes):
+                part = pl.ds(MAIN - (i + 1) * DETOUR, DETOUR)
+                pltpu.make_async_remote_copy(
+                    src_ref=blend.at[first_owner, :, part], dst_ref=relay,
+                    send_sem=s_sem, recv_sem=relay_sem.at[0],
+                    device_id=(at, source_rank + 1), device_id_type=MESH,
+                ).start()
+
+        send(first_owner, 1, source, less=len(routes) * DETOUR)
         send(first_owner, 1, jnp.logical_not(source))
     else:
         for i in range(1, PIECES - 1):
@@ -508,11 +511,15 @@
         @pl.when(jnp.logical_and(relays, low))
         def _():
             await_piece(relay, relay_sem.at[0])
-            pltpu.make_async_remote_copy(
-                src_ref=relay, dst_ref=recv.at[source_rank, :, pl.ds(MAIN - DETOUR, DETOUR)],
-                send_sem=relay_sem.at[1], recv_sem=r_sem.at[2],
-                device_id=(0, 0), device_id_type=MESH,
-            ).start()
+            for i, at in enumerate(routes):
+                @pl.when(g == at)
+                def _():
+                    part = pl.ds(MAIN - (i + 1) * DETOUR, DETOUR)
+                    pltpu.make_async_remote_copy(
+                        src_ref=relay, dst_ref=recv.at[source_rank, :, part],
+                        send_sem=relay_sem.at[1], recv_sem=r_sem.at[2],
+                        device_id=(0, 0), device_id_type=MESH,
+                    ).start()
 
     def spans(k, i):
         solo_at = pair_start(k // 2) + (k % 2) * (SOLO + 2 * shared)

time: 16.1 us -> 15.9 us (0.988)
  no operation moved by 1% of the time
where the time goes in v6:
time: 15.9 us; the launch traced here: 15.7 us
  Pallas kernels  14.8 us (93%)
  local copies, waits for them, and re-layouts  0.94 us (6%)
    pallas_call x1, Pallas kernels, shards(): pl.pallas_call(functools.partial(kernel, groups, n, per, depth, tile_rows...  14.8 us
    unnamed x1, local copies, waits for them, and re-layouts  0.94 us

profile of v6, /device:TPU:1, one launch (start us, length us, event | category | flops | bytes accessed | tf_op | source)
XLA Modules:
  0.0 15.7 jit_solution(14480386911444877358)
XLA Ops:
  0.0 14.8 %shard_map.37 = bf16[946,4,128]{2,1,0:T(4,128)(2,1)S(1)} custom-call(s32[2,32]{1,0:T(2,128)} %bitcast.5, s32[3,32]{1,0:T(4,128)} %bitcast.4, bf16[1,20,256,128]{3,2,1,0:T(8,128)(2,1)} %tile_ref.1), custom_call_target="tpu_custom_call" | custom-call | tf_op jit(solution)/shard_map/pallas_call | solution.py:618
  14.8 0.9 %copy.5 = bf16[4,946,128]{2,0,1:T(4,128)(2,1)} copy(bf16[4,946,128]{2,0,1:T(4,128)(2,1)S(1)} %bitcast.3) | data formatting | bytes 1937408

commit v7 on v6

--- a/solution.py
+++ b/solution.py
@@ -107,7 +107,8 @@
 
     routes = sorted({stride, 1}, reverse=True)
     detour = direct and groups > stride
-    relays = jnp.logical_and(functools.reduce(jnp.logical_or, [g == at for at in routes]), odd)
+    carries = functools.reduce(jnp.logical_or, [g == at for at in routes])
+    relays = jnp.logical_and(carries, odd)
     source_rank = n // 2
     source = jnp.logical_and(g == 0, r == source_rank) if detour else False
     if detour:
@@ -344,28 +345,31 @@
 
     lerps(coef_lead, 0, cut[1], start_solo, lead_start, lead_rows)
     weights(0, cut[1], start_solo)
-    await_piece(lead, load_sem.at[0])
-    not_far = jnp.logical_not(gets_far)
-    first_when = True if far_free else not_far
-    held_back = jnp.logical_and(jnp.logical_and(high, odd), gets_far) if direct else False
-    blend_owner(first_owner, 0, cut[1], (lead, head_start, head_planes - 2, coef_lead))
-    pl.semaphore_wait(barrier, greeted)
-    send(first_owner, 0, first_when)
-
-    @pl.when(jnp.logical_and(has_below, low))
-    def _():
-        pl.semaphore_signal(above_sem, inc=1, device_id=(g - 1, r), device_id_type=MESH)
-
-    if direct:
-        @pl.when(jnp.logical_and(has_above, high))
-        def _():
-            pl.semaphore_signal(below_sem, inc=1, device_id=(g + 1, r), device_id_type=MESH)
-
     for at, count, start in parts:
         lerps(coef, at, count, start, 0, tile_rows)
     weights(cut[1], MAIN - cut[1], start_solo + cut[1])
     for at, count, start in parts[1:]:
         weights(at, count, start)
+    await_piece(lead, load_sem.at[0])
+    not_far = jnp.logical_not(gets_far)
+    first_when = True if far_free else not_far
+    held_back = False
+    if direct:
+        holds = jnp.logical_or(odd, carries) if detour else odd
+        held_back = jnp.logical_and(jnp.logical_and(high, gets_far), holds)
+    blend_owner(first_owner, 0, cut[1], (lead, head_start, head_planes - 2, coef_lead))
+    pl.semaphore_wait(barrier, greeted)
+    send(first_owner, 0, first_when)
+
+    @pl.when(jnp.logical_and(has_below, low))
+    def _():
+        pl.semaphore_signal(above_sem, inc=1, device_id=(g - 1, r), device_id_type=MESH)
+
+    if direct:
+        @pl.when(jnp.logical_and(has_above, high))
+        def _():
+            pl.semaphore_signal(below_sem, inc=1, device_id=(g + 1, r), device_id_type=MESH)
+
     await_piece(raw.at[pl.ds(0, depth)], load_sem.at[1])
     blend_owner(first_owner, cut[1], frame)
     if detour:

time: 15.9 us -> 15.9 us (level)
  no operation moved by 1% of the time
where the time goes in v7:
time: 15.9 us; the launch traced here: 15.7 us
  Pallas kernels  14.8 us (93%)
  local copies, waits for them, and re-layouts  0.94 us (6%)
    pallas_call x1, Pallas kernels, shards(): pl.pallas_call(functools.partial(kernel, groups, n, per, depth, tile_rows...  14.8 us
    unnamed x1, local copies, waits for them, and re-layouts  0.94 us

profile of v7, /device:TPU:1, one launch (start us, length us, event | category | flops | bytes accessed | tf_op | source)
XLA Modules:
  0.0 15.7 jit_solution(4333988810902372770)
XLA Ops:
  0.0 14.8 %shard_map.37 = bf16[946,4,128]{2,1,0:T(4,128)(2,1)S(1)} custom-call(s32[2,32]{1,0:T(2,128)} %bitcast.5, s32[3,32]{1,0:T(4,128)} %bitcast.4, bf16[1,20,256,128]{3,2,1,0:T(8,128)(2,1)} %tile_ref.1), custom_call_target="tpu_custom_call" | custom-call | tf_op jit(solution)/shard_map/pallas_call | solution.py:622
  14.8 0.9 %copy.5 = bf16[4,946,128]{2,0,1:T(4,128)(2,1)} copy(bf16[4,946,128]{2,0,1:T(4,128)(2,1)S(1)} %bitcast.3) | data formatting | bytes 1937408

commit v8 on v7

--- a/solution.py
+++ b/solution.py
@@ -70,7 +70,7 @@
     edge_send, far_recv, near_recv, recv, relay, rec,
     offs, fracs, rampz, table,
     small_sem, load_sem, give_sem, got_sem, es_sem, far_sem, near_sem, s_sem, r_sem, relay_sem,
-    above_sem, below_sem, clear_sem,
+    ready_sem,
 ):
     g = lax.axis_index("slab")
     r = lax.axis_index("tile")
@@ -363,12 +363,12 @@
 
     @pl.when(jnp.logical_and(has_below, low))
     def _():
-        pl.semaphore_signal(above_sem, inc=1, device_id=(g - 1, r), device_id_type=MESH)
+        pl.semaphore_signal(ready_sem, inc=1, device_id=(g - 1, r), device_id_type=MESH)
 
     if direct:
         @pl.when(jnp.logical_and(has_above, high))
         def _():
-            pl.semaphore_signal(below_sem, inc=1, device_id=(g + 1, r), device_id_type=MESH)
+            pl.semaphore_signal(ready_sem, inc=1, device_id=(g + 1, r), device_id_type=MESH)
 
     await_piece(raw.at[pl.ds(0, depth)], load_sem.at[1])
     blend_owner(first_owner, cut[1], frame)
@@ -471,15 +471,6 @@
             send(owner, i, True if direct or o in near_free else jnp.logical_not(gets_near))
     join_edge(near_side)
 
-    @pl.when(jnp.logical_and(has_above, low))
-    def _():
-        pl.semaphore_wait(above_sem, 1)
-
-    if direct:
-        @pl.when(jnp.logical_and(has_below, high))
-        def _():
-            pl.semaphore_wait(below_sem, 1)
-
     for i in range(PIECES):
         @pl.when(gets_far)
         def _():
@@ -494,9 +485,13 @@
             def _():
                 await_piece(far_recv, es_sem.at[0])
                 pl.semaphore_signal(
-                    clear_sem, inc=1, device_id=(g, partner), device_id_type=MESH
+                    ready_sem, inc=1, device_id=(g, partner), device_id_type=MESH
                 )
-                pl.semaphore_wait(clear_sem, 1)
+
+            ready = jnp.where(jnp.logical_and(has_above, low), 1, 0)
+            if direct:
+                ready = ready + jnp.where(jnp.logical_and(has_below, high), 1, 0)
+            pl.semaphore_wait(ready_sem, ready + jnp.where(sends_to(far_side), 1, 0))
 
         send_near(i)
 
@@ -649,7 +644,7 @@
                 pltpu.VMEM((round_up(PADY + frame + 8, 8), cols), f32),
                 dma((2,)), dma((2,)), dma, dma((2,)), dma((2,)),
                 dma((PIECES,)), dma((PIECES,)), dma, dma(((n // 2 - 1) * PIECES + 1,)), dma((2,)),
-                signal, signal, signal,
+                signal,
             ],
             compiler_params=pltpu.CompilerParams(collective_id=0, has_side_effects=True),
         )(offsets.T, fracs.T, tiles)

time: 15.9 us -> 15.9 us (level)
  no operation moved by 1% of the time
where the time goes in v8:
time: 15.9 us; the launch traced here: 15.7 us
  Pallas kernels  14.8 us (93%)
  local copies, waits for them, and re-layouts  0.94 us (6%)
    pallas_call x1, Pallas kernels, shards(): pl.pallas_call(functools.partial(kernel, groups, n, per, depth, tile_rows...  14.8 us
    unnamed x1, local copies, waits for them, and re-layouts  0.94 us

profile of v8, /device:TPU:1, one launch (start us, length us, event | category | flops | bytes accessed | tf_op | source)
XLA Modules:
  0.0 15.7 jit_solution(12547859772349756817)
XLA Ops:
  0.0 14.8 %shard_map.37 = bf16[946,4,128]{2,1,0:T(4,128)(2,1)S(1)} custom-call(s32[2,32]{1,0:T(2,128)} %bitcast.5, s32[3,32]{1,0:T(4,128)} %bitcast.4, bf16[1,20,256,128]{3,2,1,0:T(8,128)(2,1)} %tile_ref.1), custom_call_target="tpu_custom_call" | custom-call | tf_op jit(solution)/shard_map/pallas_call | solution.py:617
  14.8 0.9 %copy.5 = bf16[4,946,128]{2,0,1:T(4,128)(2,1)} copy(bf16[4,946,128]{2,0,1:T(4,128)(2,1)S(1)} %bitcast.3) | data formatting | bytes 1937408
